TPU v7x, 32 devices: a 4x4x1 block of a 4x4x8 slice. The times are simulated.
32 devices in a mesh: dp: 1 (over z), ep2: 4 (over y), ep: 8 (over x, core).
Axes of the slice: x: 4, y: 4, z: 1, core: 2. Of those that a mesh axis runs over, the one named last changes fastest.
The devices are a block of a 4x4x8 slice.
Arguments:
- x_tok: bfloat16 [32768, 2048], P(('dp', 'ep2', 'ep'))
- expert_ids: int32 [32768, 8], P(('dp', 'ep2', 'ep'))
- gate_w: float32 [32768, 8], P(('dp', 'ep2', 'ep'))
- w_in: bfloat16 [128, 2048, 768], P(('ep2', 'ep'))
- w_out: bfloat16 [128, 768, 2048], P(('ep2', 'ep'))
Outputs:
- output: bfloat16 [32768, 2048], P(('dp', 'ep2', 'ep'))
All inputs are finite; a program needn't handle non-finite values.
Results may differ from a plain program's by a relative error of at most 0.00112.
Values are sent between devices in bfloat16 or wider.
A program may use at most 768 MiB of HBM per device.

v0:
```python
import jax
import jax.numpy as jnp
from jax import lax
from jax.sharding import PartitionSpec as P


def slot_sizes(group_size, n_tok, n_top, experts):
    capacity = 8 * ((5 * group_size * n_tok * n_top) // (32 * experts))
    lane_max = 2 * ((n_tok * n_top) // experts) - 1
    return capacity, lane_max


def pack_rows(x_loc, flat_e, counts, offsets, capacity, lane_max):
    n_tok = x_loc.shape[0]
    n_pair = flat_e.shape[0]
    pair_order = jnp.argsort(flat_e, stable=True)
    starts = jnp.cumsum(counts) - counts
    kept_n = jnp.clip(capacity - offsets, 0, counts)
    lane_ids = jnp.arange(lane_max)
    src_pair = pair_order[jnp.minimum(starts[:, None] + lane_ids[None, :], n_pair - 1)]
    is_kept = lane_ids[None, :] < kept_n[:, None]
    send_rows = jnp.where(is_kept[:, :, None], x_loc[src_pair // (n_pair // n_tok)], jnp.zeros((), x_loc.dtype))
    sorted_rank = jnp.arange(n_pair) - starts[flat_e[pair_order]]
    pair_rank = jnp.zeros((n_pair,), jnp.int32).at[pair_order].set(sorted_rank)
    return send_rows, pair_rank, kept_n


def expert_rows(recv_rows, src_counts, src_offsets, w_a, w_b, capacity):
    group_size, e_loc, lane_max, d_model = recv_rows.shape
    range_end = src_offsets + src_counts
    totals = jnp.sum(src_counts, axis=0)
    slot_ids = jnp.arange(capacity)
    src_dev = jnp.sum((range_end[:, :, None] <= slot_ids[None, None, :]).astype(jnp.int32), axis=0)
    src_dev = jnp.minimum(src_dev, group_size - 1)
    expert_pos = jnp.arange(e_loc)[:, None]
    slot_base = jnp.take_along_axis(src_offsets.T, src_dev, axis=1)
    lane_pos = jnp.clip(slot_ids[None, :] - slot_base, 0, lane_max - 1)
    flat_pos = (src_dev * e_loc + expert_pos) * lane_max + lane_pos
    filled = slot_ids[None, :] < totals[:, None]
    gathered = recv_rows.reshape(group_size * e_loc * lane_max, d_model)[flat_pos]
    slot_rows = jnp.where(filled[:, :, None], gathered, jnp.zeros((), recv_rows.dtype))
    hidden = jax.nn.gelu(jnp.einsum('ecd,edf->ecf', slot_rows, w_a, preferred_element_type=jnp.float32), approximate=True).astype(jnp.bfloat16)
    out_rows = jnp.einsum('ecf,efd->ecd', hidden, w_b, preferred_element_type=jnp.float32).astype(jnp.bfloat16)
    back_pos = expert_pos[None] * capacity + jnp.clip(src_offsets[:, :, None] + jnp.arange(lane_max)[None, None, :], 0, capacity - 1)
    return out_rows.reshape(e_loc * capacity, d_model)[back_pos]


def combine_rows(x_loc, back_rows, flat_e, flat_gate, pair_rank, kept_n):
    n_tok, d_model = x_loc.shape
    experts, lane_max, _ = back_rows.shape
    n_top = flat_e.shape[0] // n_tok
    got_rows = back_rows.reshape(experts * lane_max, d_model)[flat_e * lane_max + pair_rank]
    weight = jnp.where(pair_rank < kept_n[flat_e], flat_gate, 0.0)
    mix_sum = jnp.sum((weight[:, None] * got_rows.astype(jnp.float32)).reshape(n_tok, n_top, d_model), axis=1)
    return (x_loc.astype(jnp.float32) + mix_sum).astype(jnp.bfloat16)


def solution(mesh):
    dev_axes = ('ep2', 'ep')
    group_size = mesh.shape['ep2'] * mesh.shape['ep']

    def local_step(x_loc, ids_loc, gate_loc, w_a, w_b):
        n_tok, d_model = x_loc.shape
        n_top = ids_loc.shape[1]
        e_loc = w_a.shape[0]
        experts = e_loc * group_size
        capacity, lane_max = slot_sizes(group_size, n_tok, n_top, experts)
        flat_e = ids_loc.reshape(-1)
        counts = jnp.bincount(flat_e, length=experts)
        src_counts = lax.all_to_all(counts.reshape(group_size, e_loc), dev_axes, 0, 0, tiled=True)
        src_offsets = jnp.cumsum(src_counts, axis=0) - src_counts
        offsets = lax.all_to_all(src_offsets, dev_axes, 0, 0, tiled=True).reshape(experts)
        send_rows, pair_rank, kept_n = pack_rows(x_loc, flat_e, counts, offsets, capacity, lane_max)
        recv_rows = lax.all_to_all(send_rows.reshape(group_size, e_loc, lane_max, d_model), dev_axes, 0, 0, tiled=True)
        out_rows = expert_rows(recv_rows, src_counts, src_offsets, w_a, w_b, capacity)
        back_rows = lax.all_to_all(out_rows, dev_axes, 0, 0, tiled=True).reshape(experts, lane_max, d_model)
        return combine_rows(x_loc, back_rows, flat_e, gate_loc.reshape(-1), pair_rank, kept_n)

    tok_spec = P(('dp', 'ep2', 'ep'), None)
    w_spec = P(dev_axes, None, None)
    return jax.shard_map(local_step, mesh=mesh, in_specs=(tok_spec, tok_spec, tok_spec, w_spec, w_spec), out_specs=tok_spec, check_vma=False)
```

profile of v0, /device:TPU:107, one launch (start us, length us, event | category | flops | bytes accessed | tf_op | source)
XLA Modules:
  0.0 3493.4 jit_solution(17394809360346971846)
XLA Ops:
  0.0 0.9 copy.36
  1.0 0.3 reshape.383
  1.3 0.7 compare_select_fusion
  1.9 57.0 %scatter_custom_fusion = s32[128]{0:T(128)S(1)} fusion(s32[8192]{0:T(1024)S(1)} %bitcast.54, s32[8192]{0:T(1024)S(1)} %broadcast.384, s32[]{:T(128)} %constant.25.clone.1), kind=kCustom, calls=%fused_computation.70 | custom fusion | flops 8192 | bytes 516 | tf_op jit(solution)/shard_map/scatter-add | solution.py:69
  59.0 12.7 all_to_all.28
  71.8 0.5 copy-done.14
  72.5 0.7 copy.44
  73.2 5.9 all-to-all-start.1
  79.1 0.3 reshape.382
  79.8 6.8 sort.17
  86.7 0.5 fusion.33
  87.2 0.6 copy-done.2
  87.9 0.2 reshape.416
  88.1 83.6 %gather_fusion.3 = s32[16256]{0:T(1024)S(1)} fusion(s32[8192]{0:T(1024)S(1)} %get-tuple-element.6, s32[16384]{0:T(1024)S(1)} %pad_clamp_fusion.2), kind=kCustom, calls=%fused_computation.3 | custom fusion | bytes 195072 | tf_op jit(solution)/shard_map/gather | solution.py:20
  171.8 0.2 gather.41
  172.0 0.2 reshape.424
  172.3 123.5 %gather_fusion.4 = bf16[16256,2048]{1,0:T(8,128)(2,1)} fusion(bf16[1024,2048]{1,0:T(8,128)(2,1)} %param.5, s32[16384]{0:T(1024)S(1)} %pad_clamp_fusion.1), kind=kCustom, calls=%fused_computation.4 | custom fusion | bytes 133234176 | tf_op jit(solution)/shard_map/gather | solution.py:22
  295.8 50.4 %gather.43 = bf16[32,4,127,2048]{3,2,1,0:T(8,128)(2,1)} reshape(bf16[16256,2048]{1,0:T(8,128)(2,1)} %gather_fusion.4) | data formatting | bytes 133169152 | tf_op jit(solution)/shard_map/gather | solution.py:22
  346.4 44.4 %broadcast_select_fusion = bf16[32,4,127,2048]{3,2,1,0:T(8,128)(2,1)} fusion(bf16[32,4,127,2048]{3,2,1,0:T(8,128)(2,1)} %gather.43, pred[32,4,127]{2,1,0:T(4,128)(4,1)S(1)} %iota_compare_fusion.1), kind=kLoop, calls=%fused_computation.13 | loop fusion | flops 33292288 | bytes 133185408 | tf_op jit(solution)/shard_map/jit(_where)/select_n | solution.py:22
  390.7 81.8 %copy.46 = bf16[32,4,127,2048]{3,1,2,0:T(4,128)(2,1)} copy(bf16[32,4,127,2048]{3,2,1,0:T(8,128)(2,1)} %broadcast_select_fusion) | data formatting | bytes 133169152 | tf_op jit(solution)/shard_map/jit(_where)/select_n | solution.py:22
  472.5 7.1 all-to-all-start.2
  479.7 0.3 convert_reduce_fusion
  480.1 68.2 %gather_fusion.8 = s32[10240]{0:T(1024)S(1)} fusion(s32[4,32]{0,1:T(8,128)S(1)} %bitcast.47, s32[10240]{0:T(1024)S(1)} %reshape.454), kind=kCustom, calls=%fused_computation.8 | custom fusion | bytes 163840 | tf_op jit(solution)/shard_map/jit(take_along_axis)/gather | solution.py:36
  548.5 0.2 reshape.440
  548.8 0.6 pad_clamp_fusion
  549.5 0.7 iota_compare_fusion.2
  550.1 819.1 %all-to-all-done.2 = bf16[32,4,127,2048]{3,1,2,0:T(4,128)(2,1)} async-done(((bf16[32,4,127,2048]{3,1,2,0:T(4,128)(2,1)}), bf16[32,4,127,2048]{3,1,2,0:T(4,128)(2,1)}, u32[]{:S(2)}, u32[]{:S(2)}) %all-to-all-start.2) | async-done | bytes 66584608 | tf_op jit(solution)/shard_map/all_to_all | solution.py:74
  1369.3 56.7 %copy.47 = bf16[32,4,127,2048]{3,2,1,0:T(8,128)(2,1)} copy(bf16[32,4,127,2048]{3,1,2,0:T(4,128)(2,1)} %all-to-all-done.2) | data formatting | bytes 133169152 | tf_op jit(solution)/shard_map/all_to_all | solution.py:74
  1426.0 51.4 %reshape.387 = bf16[16256,2048]{1,0:T(8,128)(2,1)} reshape(bf16[32,4,127,2048]{3,2,1,0:T(8,128)(2,1)} %copy.47) | data formatting | bytes 133169152 | tf_op jit(solution)/shard_map/reshape | solution.py:40
  1477.4 379.4 %gather_fusion.5 = bf16[10240,2048]{1,0:T(8,128)(2,1)} fusion(bf16[16256,2048]{1,0:T(8,128)(2,1)} %reshape.387, s32[10240]{0:T(1024)S(1)} %broadcast_clamp_fusion), kind=kCustom, calls=%fused_computation.5 | custom fusion | bytes 83927040 | tf_op jit(solution)/shard_map/gather | solution.py:40
  1856.8 47.7 %fusion.11.clone.4 = bf16[4,2560,768]{2,1,0:T(8,128)(2,1)} fusion(bf16[4,2048,768]{2,1,0:T(8,128)(2,1)} %param.8, bf16[4,2560,2048]{2,1,0:T(8,128)(2,1)} %bitcast.49, pred[4,2560]{1,0:T(4,128)(4,1)S(1)} %copy-done.20), kind=kOutput, calls=%fused_computation.26.clone.clone.clone.1 | convolution fusion | flops 32304005120 | bytes 70264832 | tf_op jit(solution)/shard_map/ecd,edf->ecf/dot_general | solution.py:42
  1904.5 42.5 %convolution_convert_fusion = bf16[4,2560,2048]{2,1,0:T(8,128)(2,1)} fusion(bf16[4,768,2048]{2,1,0:T(8,128)(2,1)} %param.9, bf16[4,2560,768]{2,1,0:T(8,128)(2,1)} %fusion.11.clone.4), kind=kOutput, calls=%fused_computation.18 | convolution fusion | flops 32233226240 | bytes 70254592 | tf_op jit(solution)/shard_map/ecf,efd->ecd/dot_general | solution.py:43
  1947.1 181.6 %gather_fusion.6 = bf16[16256,2048]{1,0:T(8,128)(2,1)} fusion(bf16[10240,2048]{1,0:T(8,128)(2,1)} %bitcast.48, s32[16384]{0:T(1024)S(1)} %copy-done.9), kind=kCustom, calls=%fused_computation.6 | custom fusion | bytes 133234176 | tf_op jit(solution)/shard_map/gather | solution.py:45
  2128.7 50.4 %reshape.439 = bf16[32,4,127,2048]{3,2,1,0:T(8,128)(2,1)} reshape(bf16[16256,2048]{1,0:T(8,128)(2,1)} %gather_fusion.6) | data formatting | bytes 133169152 | tf_op jit(solution)/shard_map/gather | solution.py:45
  2179.1 81.8 %copy.50 = bf16[32,4,127,2048]{3,1,2,0:T(4,128)(2,1)} copy(bf16[32,4,127,2048]{3,2,1,0:T(8,128)(2,1)} %reshape.439) | data formatting | bytes 133169152 | tf_op jit(solution)/shard_map/gather | solution.py:45
  2260.8 5.5 all-to-all-start.3
  2266.4 45.5 %gather_fusion = s32[8192]{0:T(1024)S(1)} fusion(s32[8192]{0:T(1024)S(1)} %copy-done.7, s32[8192]{0:T(1024)S(1)} %get-tuple-element.9), kind=kCustom, calls=%fused_computation | custom fusion | bytes 98304 | tf_op jit(solution)/shard_map/gather | solution.py:23
  2312.2 0.3 reshape.386
  2312.5 48.9 %gather_fusion.1 = s32[8192]{0:T(1024)S(1)} fusion(s32[128]{0:T(128)S(1)} %copy-done.3, s32[8192]{0:T(1024)S(1)} %broadcast_clamp_fusion.2), kind=kCustom, calls=%fused_computation.1 | custom fusion | bytes 98304 | tf_op jit(solution)/shard_map/gather | solution.py:23
  2361.4 48.9 %gather_fusion.2 = s32[8192]{0:T(1024)S(1)} fusion(s32[128]{0:T(128)S(1)} %copy-done.1, s32[8192]{0:T(1024)S(1)} %broadcast_clamp_fusion.1), kind=kCustom, calls=%fused_computation.2 | custom fusion | bytes 98304 | tf_op jit(solution)/shard_map/gather | solution.py:53
  2410.3 30.5 scatter_custom_fusion.1
  2440.8 1.1 mul.72
  2441.9 712.2 %all-to-all-done.3 = bf16[32,4,127,2048]{3,1,2,0:T(4,128)(2,1)} async-done(((bf16[32,4,127,2048]{3,1,2,0:T(4,128)(2,1)}), bf16[32,4,127,2048]{3,1,2,0:T(4,128)(2,1)}, u32[]{:S(2)}, u32[]{:S(2)}) %all-to-all-start.3) | async-done | bytes 66584608 | tf_op jit(solution)/shard_map/all_to_all | solution.py:76
  3154.2 56.7 %copy.51 = bf16[32,4,127,2048]{3,2,1,0:T(8,128)(2,1)} copy(bf16[32,4,127,2048]{3,1,2,0:T(4,128)(2,1)} %all-to-all-done.3) | data formatting | bytes 133169152 | tf_op jit(solution)/shard_map/all_to_all | solution.py:76
  3210.9 51.4 %reshape_reshape.3 = bf16[16256,2048]{1,0:T(8,128)(2,1)} reshape(bf16[32,4,127,2048]{3,2,1,0:T(8,128)(2,1)} %copy.51) | data formatting | bytes 133169152 | tf_op jit(solution)/shard_map/reshape;reshape | solution.py:52
  3262.3 191.2 %gather_fusion.7 = bf16[8192,2048]{1,0:T(8,128)(2,1)} fusion(bf16[16256,2048]{1,0:T(8,128)(2,1)} %reshape_reshape.3, s32[8192]{0:T(1024)S(1)} %fusion.22), kind=kCustom, calls=%fused_computation.7 | custom fusion | bytes 67141632 | tf_op jit(solution)/shard_map/gather | solution.py:52
  3453.6 31.1 fusion
  3484.6 8.3 add_convert_fusion
  (78 shorter events, 2.0 us)
Async XLA Ops:
  71.7 0.6 copy-start.14
  72.4 0.8 copy-start.10
  72.5 0.8 copy-start.12
  72.5 0.7 copy-start.18
  73.2 13.3 all-to-all-start.1
  79.4 92.4 %copy-start.6 = (s32[8192]{0:T(1024)}, s32[8192]{0:T(1024)S(1)}, u32[]{:S(2)}) copy-start(s32[8192]{0:T(1024)S(1)} %reshape.382) | copy-start | bytes 98308
  86.6 85.2 %copy-start.4 = (s32[8192]{0:T(1024)}, s32[8192]{0:T(1024)S(1)}, u32[]{:S(2)}) copy-start(s32[8192]{0:T(1024)S(1)} %get-tuple-element.6) | copy-start | bytes 98308
  87.2 0.6 copy-start.2
  295.8 50.4 %copy-start = (s32[128]{0:T(128)S(1)}, s32[128]{0:T(128)}, u32[]{:S(2)}) copy-start(s32[128]{0:T(128)} %get-tuple-element.11) | copy-start | bytes 1540
  472.5 7.2 copy-start.11
  472.5 7.2 copy-start.13
  472.5 7.2 copy-start.19
  472.5 896.7 %all-to-all-start.2 = ((bf16[32,4,127,2048]{3,1,2,0:T(4,128)(2,1)}), bf16[32,4,127,2048]{3,1,2,0:T(4,128)(2,1)}, u32[]{:S(2)}, u32[]{:S(2)}) async-start(bf16[32,4,127,2048]{3,1,2,0:T(4,128)(2,1)} %copy.46), calls=%async_computation.2 | async-start | bytes 133169152 | tf_op jit(solution)/shard_map/all_to_all | solution.py:74
  479.6 69.1 %copy-start.15 = (s32[32,1,4]{2,1,0:T(1,128)S(1)}, s32[32,1,4]{2,1,0:T(1,128)}, u32[]{:S(2)}) copy-start(s32[32,1,4]{2,1,0:T(1,128)} %copy-done.14) | copy-start | bytes 1540
  1477.4 379.4 %copy-start.20 = (pred[4,2560]{1,0:T(4,128)(4,1)S(1)}, pred[4,2560]{1,0:T(4,128)(4,1)}, u32[]{:S(2)}) copy-start(pred[4,2560]{1,0:T(4,128)(4,1)} %iota_compare_fusion.2) | copy-start | bytes 30724
  1904.5 42.6 %copy-start.9 = (s32[16384]{0:T(1024)S(1)}, s32[16384]{0:T(1024)}, u32[]{:S(2)}) copy-start(s32[16384]{0:T(1024)} %pad_clamp_fusion) | copy-start | bytes 196612
  2260.8 5.5 copy-start.5
  2260.8 5.6 copy-start.7
  2260.8 893.3 %all-to-all-start.3 = ((bf16[32,4,127,2048]{3,1,2,0:T(4,128)(2,1)}), bf16[32,4,127,2048]{3,1,2,0:T(4,128)(2,1)}, u32[]{:S(2)}, u32[]{:S(2)}) async-start(bf16[32,4,127,2048]{3,1,2,0:T(4,128)(2,1)} %copy.50), calls=%async_computation.3 | async-start | bytes 133169152 | tf_op jit(solution)/shard_map/all_to_all | solution.py:76
  2266.4 45.6 %copy-start.17 = (f32[1024,8]{0,1:T(8,128)S(1)}, f32[1024,8]{0,1:T(8,128)}, u32[]{:S(2)}) copy-start(f32[1024,8]{0,1:T(8,128)} %param.7) | copy-start | bytes 98308
  2266.4 46.1 %copy-start.16 = (s32[8192,1]{0,1:T(1,128)S(1)}, s32[8192,1]{0,1:T(1,128)}, u32[]{:S(2)}) copy-start(s32[8192,1]{0,1:T(1,128)} %get-tuple-element.7) | copy-start | bytes 98308
  2266.4 46.1 %copy-start.3 = (s32[128]{0:T(128)S(1)}, s32[128]{0:T(128)}, u32[]{:S(2)}) copy-start(s32[128]{0:T(128)} %copy-done.2) | copy-start | bytes 1540
  2266.4 95.0 %copy-start.1 = (s32[128]{0:T(128)S(1)}, s32[128]{0:T(128)}, u32[]{:S(2)}) copy-start(s32[128]{0:T(128)} %get-tuple-element.11) | copy-start | bytes 1540
  3262.3 191.2 %copy-start.8 = (f32[1024,8]{1,0:T(8,128)S(1)}, f32[1024,8]{1,0:T(8,128)}, u32[]{:S(2)}) copy-start(f32[1024,8]{1,0:T(8,128)} %mul.72) | copy-start | bytes 98308
where the time goes:
time: 3520 us; the launch traced here: 3490 us
  local copies, waits for them, and re-layouts  1690 us (48%)
  waiting for transfers between devices  1530 us (43%)
  other arithmetic  151 us (4%)
  matrix products  90.3 us (3%)
    all_to_all x1, waiting for transfers between devices, local_step(): lax.all_to_all(send_rows.reshape(group_size, e_loc, lane_max, d_model), d...  819 us
    all_to_all x1, waiting for transfers between devices, local_step(): lax.all_to_all(out_rows, dev_axes, 0, 0, tiled=True)  712 us
    gather x1, local copies, waits for them, and re-layouts, expert_rows(): recv_rows.reshape(group_size * e_loc * lane_max, d_model)[flat_pos]  379 us
    gather x3, local copies, waits for them, and re-layouts, expert_rows(): return out_rows.reshape(e_loc * capacity, d_model)[back_pos]  314 us
    gather x1, local copies, waits for them, and re-layouts, combine_rows(): back_rows.reshape(experts * lane_max, d_model)  191 us
    gather x2, local copies, waits for them, and re-layouts, pack_rows(): x_loc[src_pair // (n_pair // n_tok)]  174 us
    gather x2, local copies, waits for them, and re-layouts, pack_rows(): sorted_rank = jnp.arange(n_pair) - starts[flat_e[pair_order]]  94.4 us
    gather x2, local copies, waits for them, and re-layouts, pack_rows(): pair_order[jnp.minimum(starts[:, None] + lane_ids[None, :], n_pair - 1)]  83.8 us
  transfers between devices with their start and end apart: 3, of which 2 were waited for; matrix products, arithmetic and copies ran while one was open for 7% of the time, Pallas kernels for 0%

commit v1 on v0

v1 whole, which is shorter than its diff:
```python
import functools
import math

import jax
import jax.numpy as jnp
from jax import lax
from jax.experimental import pallas as pl
from jax.experimental.pallas import tpu as pltpu
from jax.sharding import PartitionSpec as P

LANES = 128
CHUNKS = 4
TILE = 256
PREFIX_ROWS = 8
BF16 = jnp.bfloat16
F32 = jnp.float32
I32 = jnp.int32
HBM = pl.BlockSpec(memory_space=pl.ANY)
SMEM = pl.BlockSpec(memory_space=pltpu.SMEM)
VMEM = pl.BlockSpec(memory_space=pltpu.VMEM)
VMEM_LIMIT = 64_000_000


def capacity_of(group_size, n_tok, n_top, experts):
    return 8 * ((5 * group_size * n_tok * n_top) // (32 * experts))


def route_kernel(ids_ref, gate_ref, tok_ref, wgt_ref, cnt_ref, code_t, gate_t, tok_acc, wgt_acc):
    n_tok, n_top = ids_ref.shape
    step = n_tok // CHUNKS
    lane = lax.broadcasted_iota(I32, (n_tok, LANES), 1)
    member = jnp.zeros((n_tok, LANES), F32)
    gates = jnp.zeros((n_tok, LANES), F32)
    for j in range(n_top):
        hit = ids_ref[:, j:j + 1] == lane
        member = member + jnp.where(hit, 1.0, 0.0)
        gates = gates + jnp.where(hit, gate_ref[:, j:j + 1], 0.0)
    member_b = member.astype(BF16)
    row_block = min(n_tok, 128)
    for i in range(n_tok // row_block):
        rows = pl.ds(i * row_block, row_block)
        later = lax.broadcasted_iota(I32, (row_block, n_tok), 0) + i * row_block
        earlier = lax.broadcasted_iota(I32, (row_block, n_tok), 1)
        tri = jnp.where(earlier < later, 1.0, 0.0).astype(BF16)
        rank = jnp.dot(tri, member_b, preferred_element_type=F32)
        mem = member[i * row_block:(i + 1) * row_block]
        code_t[:, rows] = jnp.where(mem > 0.5, rank, -1.0).T
        gate_t[:, rows] = gates[i * row_block:(i + 1) * row_block].T
    total = jnp.zeros((1, LANES), F32)
    rows_out = [total]
    for k in range(CHUNKS):
        total = total + jnp.sum(member[k * step:(k + 1) * step], axis=0, keepdims=True)
        rows_out.append(total)
    while len(rows_out) < PREFIX_ROWS:
        rows_out.append(total)
    cnt_ref[...] = jnp.concatenate(rows_out, axis=0).astype(I32)
    tok_acc[...] = jnp.zeros_like(tok_acc)
    wgt_acc[...] = jnp.zeros_like(wgt_acc)
    slot = lax.broadcasted_iota(I32, (LANES, n_tok), 0).astype(F32)
    token = lax.broadcasted_iota(I32, (1, n_tok), 1).astype(F32)
    out_lane = lax.broadcasted_iota(I32, (LANES, LANES), 1)

    def one_expert(e, carry):
        hit = slot == code_t[pl.ds(e, 1), :]
        tok = jnp.sum(jnp.where(hit, token, 0.0), axis=1, keepdims=True)
        wgt = jnp.sum(jnp.where(hit, gate_t[pl.ds(e, 1), :], 0.0), axis=1, keepdims=True)
        tok_acc[...] = jnp.where(out_lane == e, tok, tok_acc[...])
        wgt_acc[...] = jnp.where(out_lane == e, wgt, wgt_acc[...])
        return carry

    lax.fori_loop(0, LANES, one_expert, 0)
    tok_ref[...] = tok_acc[...].T.astype(I32)
    wgt_ref[...] = wgt_acc[...].T


def route(ids, gate):
    n_tok = ids.shape[0]
    return pl.pallas_call(
        route_kernel,
        out_shape=(
            jax.ShapeDtypeStruct((LANES, LANES), I32),
            jax.ShapeDtypeStruct((LANES, LANES), F32),
            jax.ShapeDtypeStruct((PREFIX_ROWS, LANES), I32),
        ),
        in_specs=[VMEM, VMEM],
        out_specs=(VMEM, VMEM, VMEM),
        scratch_shapes=[
            pltpu.VMEM((LANES, n_tok), F32),
            pltpu.VMEM((LANES, n_tok), F32),
            pltpu.VMEM((LANES, LANES), F32),
            pltpu.VMEM((LANES, LANES), F32),
        ],
        cost_estimate=pl.CostEstimate(flops=2 * 10 ** 10, bytes_accessed=10 ** 6, transcendentals=0),
        name='route',
    )(ids, gate)


def list_kernel(cap, slots, n_tok, group, sub, cnt_ref, core_ref, tok_ref, src_ref, dst_ref, cs_ref, kept_ref, base_ref):
    core = core_ref[0]
    n_dst = group // 2
    step = n_tok // CHUNKS
    rows = CHUNKS + 1

    def per_expert(e, carry):
        def per_dev(g, off):
            n = cnt_ref[(g * rows + CHUNKS) * sub + e]
            kept = jnp.clip(cap - off, 0, n)

            @pl.when(g % 2 == core)
            def _():
                kept_ref[(g // 2) * sub + e] = kept
            return off + n
        return carry + lax.fori_loop(0, group, per_dev, 0) * 0

    lax.fori_loop(0, sub, per_expert, 0)

    def per_dst(i, carry):
        def add(e, acc):
            base_ref[i * sub + e] = acc
            return acc + kept_ref[i * sub + e]
        return carry + lax.fori_loop(0, sub, add, 0) * 0

    lax.fori_loop(0, n_dst, per_dst, 0)

    def expert_lists(e, carry):
        def chunk_lists(k, pos):
            cs_ref[e, k] = pos

            def segment(i, o):
                g = 2 * i + core
                kept = kept_ref[i * sub + e]
                s0 = jnp.minimum(cnt_ref[(g * rows + k) * sub + e], kept)
                s1 = jnp.minimum(cnt_ref[(g * rows + k + 1) * sub + e], kept)
                src0 = g * step - k * step
                dst0 = i * slots + base_ref[i * sub + e]

                def block(b, c):
                    for q in range(8):
                        s = s0 + b * 8 + q
                        v = tok_ref[i * sub + e, jnp.minimum(s, LANES - 1)]
                        src_ref[e, o + b * 8 + q] = src0 + v
                        dst_ref[e, o + b * 8 + q] = dst0 + s
                    return c

                n = s1 - s0
                lax.fori_loop(0, (n + 7) // 8, block, 0)
                return o + n

            return lax.fori_loop(0, n_dst, segment, pos)

        end = lax.fori_loop(0, CHUNKS, chunk_lists, 0)
        cs_ref[e, CHUNKS] = end
        return carry

    lax.fori_loop(0, sub, expert_lists, 0)


def build_lists(cnt, core, toks, cap, slots, n_tok, group, sub):
    width = LANES * (group // 2) + LANES
    return pl.pallas_call(
        functools.partial(list_kernel, cap, slots, n_tok, group, sub),
        out_shape=(
            jax.ShapeDtypeStruct((sub, width), I32),
            jax.ShapeDtypeStruct((sub, width), I32),
            jax.ShapeDtypeStruct((sub, LANES), I32),
        ),
        in_specs=[SMEM, SMEM, SMEM],
        out_specs=(SMEM, SMEM, SMEM),
        scratch_shapes=[
            pltpu.SMEM((group // 2 * sub,), I32),
            pltpu.SMEM((group // 2 * sub,), I32),
        ],
        cost_estimate=pl.CostEstimate(flops=2 * 10 ** 10, bytes_accessed=10 ** 6, transcendentals=0),
        name='row_lists',
    )(cnt, core, toks)


def rows_loop(n, fn):
    def block(b, c):
        for q in range(8):
            fn(b * 8 + q)
        return c

    def single(r, c):
        fn(r)
        return c

    full = n // 8
    lax.fori_loop(0, full, block, 0)
    lax.fori_loop(full * 8, n, single, 0)


def gelu(v):
    return 0.5 * v * (1.0 + jnp.tanh(math.sqrt(2.0 / math.pi) * (v + 0.044715 * v * v * v)))


def expert_kernel(k, first, *refs):
    if first:
        (src, dst, cs, core_ref, x_hbm, wa_own, wa_sib, wb_own, wb_sib, send,
         xbuf, obuf, wa, wb, t_e, t_base, t_cnt, gsem, ssem, wsem) = refs
    else:
        (src, dst, cs, core_ref, x_hbm, wa_own, wa_sib, wb_own, wb_sib, _, send,
         xbuf, obuf, wa, wb, t_e, t_base, t_cnt, gsem, ssem, wsem) = refs
    e_loc, d_model, _ = wa_own.shape
    sub = 2 * e_loc
    core = core_ref[0]
    sublanes = d_model // LANES

    def weight_copies(e, act):
        slot = e % 2
        q = e % e_loc

        @pl.when(e // e_loc == core)
        def _():
            act(pltpu.make_async_copy(wa_own.at[q], wa.at[slot], wsem.at[slot, 0]))
            act(pltpu.make_async_copy(wb_own.at[q], wb.at[slot], wsem.at[slot, 1]))

        @pl.when(e // e_loc != core)
        def _():
            act(pltpu.make_async_copy(wa_sib.at[q], wa.at[slot], wsem.at[slot, 0]))
            act(pltpu.make_async_copy(wb_sib.at[q], wb.at[slot], wsem.at[slot, 1]))

    weight_copies(0, lambda c: c.start())

    def plan(e, t):
        lo = cs[e, k]
        n = cs[e, k + 1] - lo

        def put(i, c):
            t_e[t + i] = e
            t_base[t + i] = lo + i * TILE
            t_cnt[t + i] = jnp.minimum(n - i * TILE, TILE)
            return c

        n_tiles = (n + TILE - 1) // TILE
        lax.fori_loop(0, n_tiles, put, 0)
        return t + n_tiles

    n_all = lax.fori_loop(0, sub, plan, 0)

    def gather_start(t):
        e, base, slot = t_e[t], t_base[t], t % 2
        rows_loop(t_cnt[t], lambda r: pltpu.make_async_copy(
            x_hbm.at[src[e, base + r]], xbuf.at[slot, r], gsem.at[slot]).start())

    def gather_wait(t):
        n, slot = t_cnt[t], t % 2
        pltpu.make_async_copy(x_hbm.at[pl.ds(0, n)], xbuf.at[slot, pl.ds(0, n)], gsem.at[slot]).wait()

    def scatter_start(t):
        e, base, slot = t_e[t], t_base[t], t % 2
        rows_loop(t_cnt[t], lambda r: pltpu.make_async_copy(
            obuf.at[slot, r], send.at[dst[e, base + r]], ssem.at[slot]).start())

    def scatter_wait(t):
        n, slot = t_cnt[t], t % 2
        pltpu.make_async_copy(obuf.at[slot, pl.ds(0, n)], send.at[pl.ds(0, n)], ssem.at[slot]).wait()

    for t in range(2):
        @pl.when(t < n_all)
        def _():
            gather_start(t)

    def one_expert(e, t_first):
        weight_copies(e, lambda c: c.wait())

        @pl.when(e + 1 < sub)
        def _():
            weight_copies(e + 1, lambda c: c.start())

        ws = e % 2
        n = cs[e, k + 1] - cs[e, k]

        def one_tile(i, t):
            slot = t % 2
            gather_wait(t)

            @pl.when(t >= 2)
            def _():
                scatter_wait(t - 2)

            rows = xbuf[slot].reshape(TILE, d_model)
            hidden = gelu(jnp.dot(rows, wa[ws], preferred_element_type=F32)).astype(BF16)
            out = jnp.dot(hidden, wb[ws], preferred_element_type=F32).astype(BF16)
            obuf[slot] = out.reshape(TILE, sublanes, LANES)

            @pl.when(t + 2 < n_all)
            def _():
                gather_start(t + 2)

            scatter_start(t)
            return t + 1

        return lax.fori_loop(0, (n + TILE - 1) // TILE, one_tile, t_first)

    lax.fori_loop(0, sub, one_expert, 0)
    for back in (2, 1):
        @pl.when(n_all >= back)
        def _():
            scatter_wait(n_all - back)


def run_experts(k, src, dst, cs, core, x_rows, wa, wa_sib, wb, wb_sib, send, send_rows):
    e_loc, d_model, ff = wa.shape
    sub = 2 * e_loc
    sublanes = d_model // LANES
    first = send is None
    ops = (src, dst, cs, core, x_rows, wa, wa_sib, wb, wb_sib) + (() if first else (send,))
    max_tiles = sub * (pl.cdiv(src.shape[1], TILE) + 1)
    flops = 4 * d_model * ff * x_rows.shape[0]
    return pl.pallas_call(
        functools.partial(expert_kernel, k, first),
        out_shape=jax.ShapeDtypeStruct((send_rows, sublanes, LANES), BF16),
        in_specs=[SMEM] * 4 + [HBM] * (len(ops) - 4),
        out_specs=HBM,
        scratch_shapes=[
            pltpu.VMEM((2, TILE, sublanes, LANES), BF16),
            pltpu.VMEM((2, TILE, sublanes, LANES), BF16),
            pltpu.VMEM((2, d_model, ff), BF16),
            pltpu.VMEM((2, ff, d_model), BF16),
            pltpu.SMEM((max_tiles,), I32),
            pltpu.SMEM((max_tiles,), I32),
            pltpu.SMEM((max_tiles,), I32),
            pltpu.SemaphoreType.DMA((2,)),
            pltpu.SemaphoreType.DMA((2,)),
            pltpu.SemaphoreType.DMA((2, 2)),
        ],
        input_output_aliases={} if first else {len(ops) - 1: 0},
        compiler_params=pltpu.CompilerParams(vmem_limit_bytes=VMEM_LIMIT),
        cost_estimate=pl.CostEstimate(flops=flops, bytes_accessed=6 * 10 ** 7, transcendentals=0),
        name='experts',
    )(*ops)


def return_kernel(rows_main, rows_last, n_y, n_x, send, recv, ssem, rsem):
    y = lax.axis_index('ep2')
    ec = lax.axis_index('ep')
    x, core = ec // 2, ec % 2
    me = y * n_x + x
    offsets = [(dy, dx) for dy in range(n_y) for dx in range(n_x) if (dy, dx) != (0, 0)]
    half_y, half_x = n_y // 2, n_x // 2
    near = lambda d, n: min(d, n - d)
    offsets.sort(key=lambda o: (near(o[0], n_y) + near(o[1], n_x), o[0] > half_y, o[1] > half_x))

    def peer(dy, dx):
        return {'ep2': lax.rem(y + dy, n_y), 'ep': lax.rem(x + dx, n_x) * 2 + core}

    barrier = pltpu.get_barrier_semaphore()
    for dy, dx in offsets:
        pl.semaphore_signal(barrier, inc=1, device_id=peer(dy, dx), device_id_type=pl.DeviceIdType.MESH)
    pl.semaphore_wait(barrier, len(offsets))

    def copy(i, dy, dx, rows):
        ty, tx = lax.rem(y + dy, n_y), lax.rem(x + dx, n_x)
        return pltpu.make_async_remote_copy(
            src_ref=send.at[ty * n_x + tx, pl.ds(0, rows)],
            dst_ref=recv.at[me, pl.ds(0, rows)],
            send_sem=ssem.at[i],
            recv_sem=rsem.at[i],
            device_id=peer(dy, dx),
            device_id_type=pl.DeviceIdType.MESH,
        )

    def sized(row, fn):
        if rows_main == rows_last:
            fn(rows_main)
            return

        @pl.when(row < n_y - 1)
        def _():
            fn(rows_main)

        @pl.when(row == n_y - 1)
        def _():
            fn(rows_last)

    for i, (dy, dx) in enumerate(offsets):
        sized(lax.rem(y + dy, n_y), lambda rows: copy(i, dy, dx, rows).start())
    for i, (dy, dx) in enumerate(offsets):
        sized(lax.rem(y + dy, n_y), lambda rows: copy(i, dy, dx, rows).wait_send())
    for i, (dy, dx) in enumerate(offsets):
        sized(y, lambda rows: copy(i, dy, dx, rows).wait_recv())


def send_back(rows_main, rows_last, cid, n_y, n_x, send):
    n = n_y * n_x - 1
    return pl.pallas_call(
        functools.partial(return_kernel, rows_main, rows_last, n_y, n_x),
        out_shape=jax.ShapeDtypeStruct(send.shape, BF16),
        in_specs=[HBM],
        out_specs=HBM,
        scratch_shapes=[pltpu.SemaphoreType.DMA((n,)), pltpu.SemaphoreType.DMA((n,))],
        compiler_params=pltpu.CompilerParams(collective_id=cid, has_side_effects=True),
        name='send_back_%d_%d' % (rows_main, rows_last),
    )(send)


def combine_kernel(tok, wgt, kept, chip_ref, recv, send, x_ref, y_ref, rbuf, acc0, acc1, acc2, acc3, sem):
    n_tok, d_model = x_ref.shape
    n_chip, slots, sublanes, _ = recv.shape
    sub = kept.shape[0] // n_chip
    accs = (acc0, acc1, acc2, acc3)
    mine = chip_ref[0]
    blk = 16

    def count(i):
        n = kept[i * sub]
        for q in range(1, sub):
            n = n + kept[i * sub + q]
        return n

    def fetch(i, act):
        slot = i % 2
        n = count(i)

        @pl.when(jnp.logical_and(i == mine, n > 0))
        def _():
            act(pltpu.make_async_copy(send.at[i, pl.ds(0, n)], rbuf.at[slot, pl.ds(0, n)], sem.at[slot]))

        @pl.when(jnp.logical_and(i != mine, n > 0))
        def _():
            act(pltpu.make_async_copy(recv.at[i, pl.ds(0, n)], rbuf.at[slot, pl.ds(0, n)], sem.at[slot]))

    fetch(0, lambda c: c.start())

    def zero(b, c):
        for acc in accs:
            acc[pl.ds(b * blk, blk)] = jnp.zeros((blk, sublanes, LANES), F32)
        return c

    lax.fori_loop(0, n_tok // blk, zero, 0)

    def one_chip(i, c):
        slot = i % 2

        @pl.when(i + 1 < n_chip)
        def _():
            fetch(i + 1, lambda d: d.start())

        fetch(i, lambda d: d.wait())

        def one_expert(q, base):
            e = i * sub + q
            n = kept[e]

            def quad(b, cc):
                for p in range(4):
                    s = b * 4 + p
                    s_in = jnp.minimum(s, LANES - 1)
                    t = jnp.where(s < n, tok[e, s_in], n_tok)
                    row = rbuf[slot, base + s].astype(F32)
                    accs[p][t] = accs[p][t] + wgt[e, s_in] * row
                return cc

            lax.fori_loop(0, (n + 3) // 4, quad, 0)
            return base + n

        lax.fori_loop(0, sub, one_expert, 0)
        return c

    lax.fori_loop(0, n_chip, one_chip, 0)

    def finish(b, c):
        rows = pl.ds(pl.multiple_of(b * blk, blk), blk)
        total = (acc0[rows] + acc1[rows]) + (acc2[rows] + acc3[rows])
        y_ref[rows, :] = (x_ref[rows, :].astype(F32) + total.reshape(blk, d_model)).astype(BF16)
        return c

    lax.fori_loop(0, n_tok // blk, finish, 0)


def combine(tok, wgt, kept, chip, recv, send, x):
    n_tok, d_model = x.shape
    n_chip, slots, sublanes, _ = recv.shape
    acc = pltpu.VMEM((n_tok + 8, sublanes, LANES), F32)
    return pl.pallas_call(
        combine_kernel,
        out_shape=jax.ShapeDtypeStruct((n_tok, d_model), BF16),
        in_specs=[SMEM, SMEM, SMEM, SMEM, HBM, HBM, VMEM],
        out_specs=VMEM,
        scratch_shapes=[
            pltpu.VMEM((2, slots + 8, sublanes, LANES), BF16),
            acc, acc, acc, acc,
            pltpu.SemaphoreType.DMA((2,)),
        ],
        compiler_params=pltpu.CompilerParams(vmem_limit_bytes=VMEM_LIMIT),
        cost_estimate=pl.CostEstimate(flops=2 * 10 ** 10, bytes_accessed=6 * 10 ** 7, transcendentals=0),
        name='combine',
    )(tok, wgt, kept, chip, recv, send, x)


def solution(mesh):
    dev_axes = ('ep2', 'ep')
    n_y, n_ep = mesh.shape['ep2'], mesh.shape['ep']
    n_x = n_ep // 2
    group = n_y * n_ep
    n_chip = n_y * n_x

    def local_step(x_loc, ids_loc, gate_loc, w_a, w_b):
        n_tok, d_model = x_loc.shape
        n_top = ids_loc.shape[1]
        e_loc = w_a.shape[0]
        sub = 2 * e_loc
        experts = e_loc * group
        cap = capacity_of(group, n_tok, n_top, experts)
        sublanes = d_model // LANES
        slots = sub * LANES
        step = n_tok // CHUNKS
        me = lax.axis_index(dev_axes)
        core, chip = me % 2, me // 2

        x3 = x_loc.reshape(n_tok, sublanes, LANES)
        chunks = [lax.all_gather(x3[k * step:(k + 1) * step], dev_axes, tiled=True) for k in range(CHUNKS)]
        swap = [(i, i ^ 1) for i in range(n_ep)]
        w_a_sib = lax.ppermute(w_a, 'ep', swap)
        w_b_sib = lax.ppermute(w_b, 'ep', swap)

        toks, wgts, cnts = route(ids_loc, gate_loc)
        info = jnp.concatenate([toks[:experts].reshape(n_chip, sub, LANES), jnp.pad(cnts, ((0, sub - PREFIX_ROWS), (0, 0)))[None]], axis=0)
        info, chunks[0] = lax.optimization_barrier((info, chunks[0]))
        every = lax.all_gather(info, dev_axes, tiled=False)
        cnt_all = every[:, n_chip, :CHUNKS + 1, :]
        my_cnt = lax.dynamic_slice(cnt_all, (0, 0, chip * sub), (group, CHUNKS + 1, sub)).reshape(-1)
        by_core = every.reshape(n_chip, 2, n_chip + 1, sub, LANES)
        my_tok = lax.dynamic_slice(by_core, (0, core, chip, 0, 0), (n_chip, 1, 1, sub, LANES)).reshape(n_chip * sub, LANES)
        core1 = core.reshape(1).astype(I32)
        src, dst, cs = build_lists(my_cnt, core1, my_tok, cap, slots, n_tok, group, sub)

        totals = cnt_all[:, CHUNKS, :experts]
        offs = jnp.cumsum(totals, axis=0) - totals
        kept = jnp.clip(cap - offs, 0, totals)
        kept_own = lax.dynamic_slice(kept, (me, 0), (1, experts)).reshape(experts)
        need = jnp.sum(kept.reshape(n_y, n_ep, n_chip, sub), axis=3)
        need_main = jnp.max(need[:n_y - 1])
        need_last = jnp.max(need[n_y - 1])

        send = None
        for k in range(CHUNKS):
            send = run_experts(k, src, dst, cs, core1, chunks[k], w_a, w_a_sib, w_b, w_b_sib, send, n_chip * slots)
        send = send.reshape(n_chip, slots, sublanes, LANES)

        tiers = [(slots * a // 64, slots * b // 64) for a, b in ((43, 32), (45, 36), (49, 36), (53, 40))] + [(slots, slots)]
        index = jnp.int32(len(tiers) - 1)
        for i in range(len(tiers) - 2, -1, -1):
            fits = jnp.logical_and(need_main <= tiers[i][0], need_last <= tiers[i][1])
            index = jnp.where(fits, jnp.int32(i), index)
        recv = lax.switch(index, [functools.partial(send_back, a, b, i, n_y, n_x) for i, (a, b) in enumerate(tiers)], send)
        return combine(toks, wgts, kept_own, chip.reshape(1).astype(I32), recv, send, x_loc)

    tok_spec = P(('dp', 'ep2', 'ep'), None)
    w_spec = P(dev_axes, None, None)
    return jax.shard_map(local_step, mesh=mesh, in_specs=(tok_spec, tok_spec, tok_spec, w_spec, w_spec), out_specs=tok_spec, check_vma=False)
```

time: 3520 us -> 1440 us (0.41)
  local copies, waits for them, and re-layouts: 1690 us -> 14.6 us
  waiting for transfers between devices: 1530 us -> 214 us
  Pallas kernels: 0 us -> 1190 us
  other arithmetic: 151 us -> 3.89 us
  matrix products: 90.3 us -> 0 us
    all_to_all x3 -> x0, waiting for transfers between devices: 1530 us -> none  [the longest x1 819 us: local_step(): lax.all_to_all(send_rows.reshape(group_size, e_loc, lane_max, d_model), d...]
    gather x15 -> x0, local copies, waits for them, and re-layouts: 1350 us -> none  [the longest x1 379 us: expert_rows(): recv_rows.reshape(group_size * e_loc * lane_max, d_model)[flat_pos]]
    pallas_call x0 -> x8, Pallas kernels: none -> 1190 us  [the longest x1 835 us: send_back(): pl.pallas_call(functools.partial(return_kernel, rows_main, rows_last, n_y...]
    all_gather x0 -> x5, waiting for transfers between devices: none -> 214 us  [the longest x4 179 us: local_step(): lax.all_gather(x3[k * step:(k + 1) * step], dev_axes, tiled=True)]
    all_to_all x5 -> x0, local copies, waits for them, and re-layouts: 114 us -> none  [the longest x1 56.7 us: local_step(): lax.all_to_all(send_rows.reshape(group_size, e_loc, lane_max, d_model), d...]
    dot_general x2 -> x0, matrix products: 90.3 us -> none  [the longest x1 47.7 us: expert_rows(): jnp.einsum('ecd,edf->ecf', slot_rows, w_a, preferred_element_type=jnp.flo...]
    select_n x5 -> x0, local copies, waits for them, and re-layouts: 82.4 us -> none  [the longest x1 81.8 us: pack_rows(): jnp.where(is_kept[:, :, None], x_loc[src_pair // (n_pair // n_tok)], jnp....]
    scatter-add x1 -> x0, other arithmetic: 57 us -> none  [local_step(): counts = jnp.bincount(flat_e, length=experts)]
  transfers between devices with their start and end apart: 3 -> 7, of which waited for: 2 -> 4; matrix products, arithmetic and copies ran while one was open for 7% -> 1% of each run, Pallas kernels for 0% -> 17%
where the time goes in v1:
time: 1440 us
  Pallas kernels  1190 us (83%)
  waiting for transfers between devices  214 us (15%)
  between operations  17.3 us (1%)
  local copies, waits for them, and re-layouts  14.6 us (1%)
    pallas_call x1, Pallas kernels, send_back(): pl.pallas_call(functools.partial(return_kernel, rows_main, rows_last, n_y...  835 us
    pallas_call x4, Pallas kernels, run_experts(): pl.pallas_call(functools.partial(expert_kernel, k, first), out_shape=jax....  180 us
    all_gather x4, waiting for transfers between devices, local_step(): lax.all_gather(x3[k * step:(k + 1) * step], dev_axes, tiled=True)  179 us
    pallas_call x1, Pallas kernels, build_lists(): pl.pallas_call(functools.partial(list_kernel, cap, slots, n_tok, group, s...  81.9 us
    pallas_call x1, Pallas kernels, combine(): pl.pallas_call(combine_kernel, out_shape=jax.ShapeDtypeStruct((n_tok, d_m...  59.9 us
    all_gather x1, waiting for transfers between devices, local_step(): every = lax.all_gather(info, dev_axes, tiled=False)  35.1 us
  transfers between devices with their start and end apart: 7, of which 4 were waited for; matrix products, arithmetic and copies ran while one was open for 1% of the time, Pallas kernels for 17%

profile of v1, /device:TPU:107, one launch (start us, length us, event | category | flops | bytes accessed | tf_op | source)
XLA Modules:
  0.0 1436.2 jit_solution(8629713854878469769)
XLA Ops:
  6.5 0.0 all-gather.7.cloned.1.call-start
  6.6 2.6 slice_bitcast_fusion
  9.1 1.2 copy.24
  10.3 0.1 all-gather.7.cloned.1.call-update
  10.4 0.1 all-gather.15.cloned.1.call-start
  10.5 1.8 copy.19.ids_ref
  12.2 1.7 copy.20.gate_ref
  14.0 28.4 %route.1 = (s32[128,128]{1,0:T(8,128)}, f32[128,128]{1,0:T(8,128)}, s32[8,128]{1,0:T(8,128)}) custom-call(s32[1024,8]{1,0:T(8,128)} %copy.19.ids_ref, f32[1024,8]{1,0:T(8,128)} %copy.20.gate_ref), custom_call_target="tpu_custom_call" | custom-call | flops 20000000000 | bytes 1000000 | tf_op jit(solution)/shard_map/route/pallas_call | solution.py:78
  42.4 1.5 pad_add_fusion
  43.8 76.0 %all-gather.7.cloned.1.call-done.refs_4_ = bf16[8192,16,128]{2,1,0:T(8,128)(2,1)} async-done(((bf16[256,16,128]{2,1,0:T(8,128)(2,1)}), bf16[8192,16,128]{2,1,0:T(8,128)(2,1)}) %all-gather.7.cloned.1.call-update) | async-done | bytes 33554448 | tf_op jit(solution)/shard_map/all_gather | solution.py:513
  119.8 0.1 all-gather.15.cloned.1.call-update
  119.9 0.1 all-gather.13.cloned.1.call-start
  120.0 1.2 copy.27
  121.2 0.1 all-gather.13.cloned.1.call-update
  121.2 0.1 all-gather.11.cloned.1.call-start
  121.3 1.3 copy.26
  122.6 0.1 all-gather.11.cloned.1.call-update
  122.7 0.1 all-gather.9.cloned.1.call-start
  122.7 1.2 copy.25
  123.9 0.1 all-gather.9.cloned.1.call-update
  124.0 0.4 collective-permute-start
  124.4 0.2 collective-permute-start.1
  124.6 35.1 %all-gather.15.cloned.1.call-done = s32[544,8,128]{2,1,0:T(8,128)} async-done(((s32[17,8,128]{2,1,0:T(8,128)}), s32[544,8,128]{2,1,0:T(8,128)}) %all-gather.15.cloned.1.call-update) | async-done | bytes 2228240 | tf_op jit(solution)/shard_map/all_gather | solution.py:521
  159.8 0.9 slice.48
  160.7 0.1 constant_dynamic-slice_fusion
  160.8 0.1 copy.22
  160.9 0.7 reshape.56.cnt_ref
  161.6 0.1 reduce_window_sum.13
  161.6 0.2 reduce_window_sum.14
  161.8 0.2 squeeze.11
  162.0 0.6 minimum_reduce_fusion
  162.6 0.6 slice_reduce_fusion
  164.4 0.6 slice_reduce_fusion.1
  167.8 0.5 minimum_bitcast_fusion.kept
  168.3 1.5 dynamic-slice_bitcast_fusion.tok_ref
  169.8 81.9 %row_lists.1 = (s32[8,2176]{1,0:T(8,128)}, s32[8,2176]{1,0:T(8,128)}, s32[8,128]{1,0:T(8,128)}) custom-call(s32[1280]{0:T(1024)} %reshape.56.cnt_ref, s32[1]{0:T(128)} %bitcast.7.core_ref.refs_3_, s32[128,128]{1,0:T(8,128)} %dynamic-slice_bitcast_fusion.tok_ref), custom_call_target="tpu_custom_call" | custom-call | flops 20000000000 | bytes 1000000 | tf_op jit(solution)/shard_map/row_lists/pallas_call | solution.py:160
  251.7 0.0 collective-permute-done.refs_6_
  251.7 0.0 collective-permute-done.1.refs_8_
  251.7 43.8 %experts.4.refs_9_ = bf16[16384,16,128]{2,1,0:T(8,128)(2,1)} custom-call(s32[8,2176]{1,0:T(8,128)} %get-tuple-element.28.refs_0_, s32[8,2176]{1,0:T(8,128)} %get-tuple-element.29.refs_1_, s32[8,128]{1,0:T(8,128)} %get-tuple-element.30.refs_2_, s32[1]{0:T(128)} %bitcast.7.core_ref.refs_3_, bf16[8192,16,128]{2,1,0:T(8,128)(2,1)} %all-gather.7.cloned.1.call-done.refs_4_, ...), custom_call_target="tpu_custom_call" | custom-call | flops 51539607552 | bytes 60000000 | tf_op jit(solution)/shard_map/experts/pallas_call | solution.py:311
  295.4 0.0 all-gather.13.cloned.1.call-done.refs_4_
  295.5 43.9 %experts.5.refs_9_ = bf16[16384,16,128]{2,1,0:T(8,128)(2,1)} custom-call(s32[8,2176]{1,0:T(8,128)} %get-tuple-element.28.refs_0_, s32[8,2176]{1,0:T(8,128)} %get-tuple-element.29.refs_1_, s32[8,128]{1,0:T(8,128)} %get-tuple-element.30.refs_2_, s32[1]{0:T(128)} %bitcast.7.core_ref.refs_3_, ...), custom_call_target="tpu_custom_call", output_to_operand_aliasing={{}: (9, {})} | custom-call | flops 51539607552 | bytes 60000000 | tf_op jit(solution)/shard_map/experts/pallas_call | solution.py:311
  339.4 39.4 %all-gather.11.cloned.1.call-done.refs_4_ = bf16[8192,16,128]{2,1,0:T(8,128)(2,1)} async-done(((bf16[256,16,128]{2,1,0:T(8,128)(2,1)}), bf16[8192,16,128]{2,1,0:T(8,128)(2,1)}) %all-gather.11.cloned.1.call-update) | async-done | bytes 33554448 | tf_op jit(solution)/shard_map/all_gather | solution.py:513
  378.8 46.3 %experts.6.refs_9_ = bf16[16384,16,128]{2,1,0:T(8,128)(2,1)} custom-call(s32[8,2176]{1,0:T(8,128)} %get-tuple-element.28.refs_0_, s32[8,2176]{1,0:T(8,128)} %get-tuple-element.29.refs_1_, s32[8,128]{1,0:T(8,128)} %get-tuple-element.30.refs_2_, s32[1]{0:T(128)} %bitcast.7.core_ref.refs_3_, ...), custom_call_target="tpu_custom_call", output_to_operand_aliasing={{}: (9, {})} | custom-call | flops 51539607552 | bytes 60000000 | tf_op jit(solution)/shard_map/experts/pallas_call | solution.py:311
  425.1 63.1 %all-gather.9.cloned.1.call-done.refs_4_ = bf16[8192,16,128]{2,1,0:T(8,128)(2,1)} async-done(((bf16[256,16,128]{2,1,0:T(8,128)(2,1)}), bf16[8192,16,128]{2,1,0:T(8,128)(2,1)}) %all-gather.9.cloned.1.call-update) | async-done | bytes 33554448 | tf_op jit(solution)/shard_map/all_gather | solution.py:513
  488.2 46.3 %experts.7 = bf16[16384,16,128]{2,1,0:T(8,128)(2,1)} custom-call(s32[8,2176]{1,0:T(8,128)} %get-tuple-element.28.refs_0_, s32[8,2176]{1,0:T(8,128)} %get-tuple-element.29.refs_1_, s32[8,128]{1,0:T(8,128)} %get-tuple-element.30.refs_2_, s32[1]{0:T(128)} %bitcast.7.core_ref.refs_3_, ...), custom_call_target="tpu_custom_call", output_to_operand_aliasing={{}: (9, {})} | custom-call | flops 51539607552 | bytes 60000000 | tf_op jit(solution)/shard_map/experts/pallas_call | solution.py:311
  534.6 835.2 %conditional.1 = (bf16[16,1024,16,128]{3,2,1,0:T(8,128)(2,1)}) conditional(s32[]{:T(128)} %clamp.3, bf16[16,1024,16,128]{3,2,1,0:T(8,128)(2,1)} %bitcast.10.send, bf16[16,1024,16,128]{3,2,1,0:T(8,128)(2,1)} %bitcast.10.send, bf16[16,1024,16,128]{3,2,1,0:T(8,128)(2,1)} %bitcast.10.send, ...), branch_computations={%region_4.5_spmd, %region_5.6_spmd, %region_6.7_spmd, %region_7.8_... | conditional | bytes 8 | solution.py:547
  534.6 835.1 %send_back_848_640.1 = bf16[16,1024,16,128]{3,2,1,0:T(8,128)(2,1)} custom-call(bf16[16,1024,16,128]{3,2,1,0:T(8,128)(2,1)} %send.3), custom_call_target="tpu_custom_call" | custom-call | tf_op jit(solution)/shard_map/cond/branch_3_fun/send_back_848_640/pallas_call | solution.py:387
  1369.7 59.9 %combine.1 = bf16[1024,2048]{1,0:T(8,128)(2,1)} custom-call(s32[128,128]{1,0:T(8,128)} %get-tuple-element.24.tok, f32[128,128]{1,0:T(8,128)} %get-tuple-element.25.wgt, s32[128]{0:T(128)} %minimum_bitcast_fusion.kept, s32[1]{0:T(128)} %bitcast.6.chip_ref, bf16[16,1024,16,128]{3,2,1,0:T(8,128)(2,1)} %get-tuple-element.38.recv, ...), custom_call_target="tpu_custom_call" | custom-call | flops 20000000000 | bytes 60000000 | tf_op jit(solution)/shard_map/combine/pallas_call | solution.py:476
  (3 shorter events, 0.0 us)
Async XLA Ops:
  6.5 113.3 %all-gather.7.cloned.1.call-start = ((), (), s32[]{:S(2)}) async-start(), calls=%async_computation | async-start | bytes 34603008 | tf_op jit(solution)/shard_map/all_gather | solution.py:513
  10.4 149.3 %all-gather.15.cloned.1.call-start = ((), (), s32[]{:S(2)}) async-start(), calls=%async_computation.4 | async-start | bytes 2297856 | tf_op jit(solution)/shard_map/all_gather | solution.py:521
  119.9 175.6 %all-gather.13.cloned.1.call-start = ((), (), s32[]{:S(2)}) async-start(), calls=%async_computation.3 | async-start | bytes 34603008 | tf_op jit(solution)/shard_map/all_gather | solution.py:513
  121.2 257.5 %all-gather.11.cloned.1.call-start = ((), (), s32[]{:S(2)}) async-start(), calls=%async_computation.2 | async-start | bytes 34603008 | tf_op jit(solution)/shard_map/all_gather | solution.py:513
  122.7 365.6 %all-gather.9.cloned.1.call-start = ((), (), s32[]{:S(2)}) async-start(), calls=%async_computation.1 | async-start | bytes 34603008 | tf_op jit(solution)/shard_map/all_gather | solution.py:513
  124.0 127.7 %collective-permute-start = (bf16[4,2048,768]{2,1,0:T(8,128)(2,1)}, bf16[4,2048,768]{2,1,0:T(8,128)(2,1)}, u32[]{:S(2)}, u32[]{:S(2)}) collective-permute-start(bf16[4,2048,768]{2,1,0:T(8,128)(2,1)} %refs_5_.7), channel_id=1, source_target_pairs={{0,1},{1,0},{2,3},{3,2},{4,5},{5,4},{6,7},{7,6},{8,9},{9,8},{10,11... | collective-permute-start | bytes 37748744 | tf_op jit(solution)/shard_map/ppermute | solution.py:515
  124.4 127.3 %collective-permute-start.1 = (bf16[4,768,2048]{2,1,0:T(8,128)(2,1)}, bf16[4,768,2048]{2,1,0:T(8,128)(2,1)}, u32[]{:S(2)}, u32[]{:S(2)}) collective-permute-start(bf16[4,768,2048]{2,1,0:T(8,128)(2,1)} %refs_7_.7), channel_id=1, source_target_pairs={{0,1},{1,0},{2,3},{3,2},{4,5},{5,4},{6,7},{7,6},{8,9},{9,8},{10,11... | collective-permute-start | bytes 37748744 | tf_op jit(solution)/shard_map/ppermute | solution.py:516
Sparse Core Ops, SparseCore 0:
  10.5 109.2 all-gather.6
  122.0 37.7 all-gather.14
  161.8 107.4 all-gather.12
  271.3 107.4 all-gather.10
  380.7 107.4 all-gather.8

commit v2 on v1

--- a/solution.py
+++ b/solution.py
@@ -9,7 +9,8 @@
 from jax.sharding import PartitionSpec as P
 
 LANES = 128
-CHUNKS = 4
+CHUNK_UNITS = 16
+CHUNK_ENDS = (0, 4, 12, 16)
 TILE = 256
 PREFIX_ROWS = 8
 BF16 = jnp.bfloat16
@@ -25,9 +26,8 @@
     return 8 * ((5 * group_size * n_tok * n_top) // (32 * experts))
 
 
-def route_kernel(ids_ref, gate_ref, tok_ref, wgt_ref, cnt_ref, code_t, gate_t, tok_acc, wgt_acc):
+def route_kernel(bounds, ids_ref, gate_ref, tok_ref, wgt_ref, cnt_ref, code_t, gate_t, tok_acc, wgt_acc):
     n_tok, n_top = ids_ref.shape
-    step = n_tok // CHUNKS
     lane = lax.broadcasted_iota(I32, (n_tok, LANES), 1)
     member = jnp.zeros((n_tok, LANES), F32)
     gates = jnp.zeros((n_tok, LANES), F32)
@@ -48,8 +48,8 @@
         gate_t[:, rows] = gates[i * row_block:(i + 1) * row_block].T
     total = jnp.zeros((1, LANES), F32)
     rows_out = [total]
-    for k in range(CHUNKS):
-        total = total + jnp.sum(member[k * step:(k + 1) * step], axis=0, keepdims=True)
+    for lo, hi in zip(bounds[:-1], bounds[1:]):
+        total = total + jnp.sum(member[lo:hi], axis=0, keepdims=True)
         rows_out.append(total)
     while len(rows_out) < PREFIX_ROWS:
         rows_out.append(total)
@@ -73,10 +73,10 @@
     wgt_ref[...] = wgt_acc[...].T
 
 
-def route(ids, gate):
+def route(ids, gate, bounds):
     n_tok = ids.shape[0]
     return pl.pallas_call(
-        route_kernel,
+        functools.partial(route_kernel, bounds),
         out_shape=(
             jax.ShapeDtypeStruct((LANES, LANES), I32),
             jax.ShapeDtypeStruct((LANES, LANES), F32),
@@ -95,22 +95,29 @@
     )(ids, gate)
 
 
-def list_kernel(cap, slots, n_tok, group, sub, cnt_ref, core_ref, tok_ref, src_ref, dst_ref, cs_ref, kept_ref, base_ref):
-    core = core_ref[0]
+def list_kernel(cap, slots, bounds, group, sub, place_ref, info_ref, src_ref, start_ref, len_ref, dst_ref, cs_ref, kept_ref, base_ref):
+    core, chip = place_ref[0], place_ref[1]
     n_dst = group // 2
-    step = n_tok // CHUNKS
-    rows = CHUNKS + 1
+    n_chunk = len(bounds) - 1
+    dev_words = (sub + PREFIX_ROWS) * LANES
+    width = src_ref.shape[0] // sub
+
+    def count(g, k, e):
+        return info_ref[g * dev_words + (sub + k) * LANES + chip * sub + e]
 
     def per_expert(e, carry):
-        def per_dev(g, off):
-            n = cnt_ref[(g * rows + CHUNKS) * sub + e]
-            kept = jnp.clip(cap - off, 0, n)
-
-            @pl.when(g % 2 == core)
-            def _():
-                kept_ref[(g // 2) * sub + e] = kept
-            return off + n
-        return carry + lax.fori_loop(0, group, per_dev, 0) * 0
+        def per_dev(i, off):
+            for c in range(2):
+                n = count(2 * i + c, n_chunk, e)
+                kept = jnp.clip(cap - off, 0, n)
+                off = off + n
+
+                @pl.when(core == c)
+                def _():
+                    kept_ref[i * sub + e] = kept
+            return off
+        lax.fori_loop(0, n_dst, per_dev, 0)
+        return carry
 
     lax.fori_loop(0, sub, per_expert, 0)
 
@@ -118,61 +125,67 @@
         def add(e, acc):
             base_ref[i * sub + e] = acc
             return acc + kept_ref[i * sub + e]
-        return carry + lax.fori_loop(0, sub, add, 0) * 0
+        lax.fori_loop(0, sub, add, i * slots)
+        return carry
 
     lax.fori_loop(0, n_dst, per_dst, 0)
 
     def expert_lists(e, carry):
-        def chunk_lists(k, pos):
-            cs_ref[e, k] = pos
+        pos = e * width
+        for k in range(n_chunk):
+            cs_ref[e * (n_chunk + 1) + k] = pos
+            size = bounds[k + 1] - bounds[k]
 
             def segment(i, o):
                 g = 2 * i + core
                 kept = kept_ref[i * sub + e]
-                s0 = jnp.minimum(cnt_ref[(g * rows + k) * sub + e], kept)
-                s1 = jnp.minimum(cnt_ref[(g * rows + k + 1) * sub + e], kept)
-                src0 = g * step - k * step
-                dst0 = i * slots + base_ref[i * sub + e]
+                s0 = jnp.minimum(count(g, k, e), kept)
+                n = jnp.minimum(count(g, k + 1, e), kept) - s0
+                j = (e * n_chunk + k) * n_dst + i
+                start_ref[j] = o
+                len_ref[j] = n
+                dst_ref[j] = base_ref[i * sub + e] + s0
+                src0 = g * size - bounds[k]
+                tok0 = g * dev_words + e * LANES + s0
 
                 def block(b, c):
+                    vals = [info_ref[tok0 + b * 8 + q] for q in range(8)]
                     for q in range(8):
-                        s = s0 + b * 8 + q
-                        v = tok_ref[i * sub + e, jnp.minimum(s, LANES - 1)]
-                        src_ref[e, o + b * 8 + q] = src0 + v
-                        dst_ref[e, o + b * 8 + q] = dst0 + s
+                        src_ref[o + b * 8 + q] = src0 + vals[q]
                     return c
 
-                n = s1 - s0
                 lax.fori_loop(0, (n + 7) // 8, block, 0)
                 return o + n
 
-            return lax.fori_loop(0, n_dst, segment, pos)
-
-        end = lax.fori_loop(0, CHUNKS, chunk_lists, 0)
-        cs_ref[e, CHUNKS] = end
+            pos = lax.fori_loop(0, n_dst, segment, pos)
+        cs_ref[e * (n_chunk + 1) + n_chunk] = pos
         return carry
 
     lax.fori_loop(0, sub, expert_lists, 0)
 
 
-def build_lists(cnt, core, toks, cap, slots, n_tok, group, sub):
-    width = LANES * (group // 2) + LANES
+def build_lists(place, info, cap, slots, bounds, group, sub):
+    n_dst, n_chunk = group // 2, len(bounds) - 1
+    width = LANES * n_dst + 8
+    segs = sub * n_chunk * n_dst
     return pl.pallas_call(
-        functools.partial(list_kernel, cap, slots, n_tok, group, sub),
+        functools.partial(list_kernel, cap, slots, bounds, group, sub),
         out_shape=(
-            jax.ShapeDtypeStruct((sub, width), I32),
-            jax.ShapeDtypeStruct((sub, width), I32),
-            jax.ShapeDtypeStruct((sub, LANES), I32),
+            jax.ShapeDtypeStruct((sub * width,), I32),
+            jax.ShapeDtypeStruct((segs,), I32),
+            jax.ShapeDtypeStruct((segs,), I32),
+            jax.ShapeDtypeStruct((segs,), I32),
+            jax.ShapeDtypeStruct((sub * (n_chunk + 1),), I32),
         ),
-        in_specs=[SMEM, SMEM, SMEM],
-        out_specs=(SMEM, SMEM, SMEM),
+        in_specs=[SMEM, SMEM],
+        out_specs=(SMEM,) * 5,
         scratch_shapes=[
-            pltpu.SMEM((group // 2 * sub,), I32),
-            pltpu.SMEM((group // 2 * sub,), I32),
+            pltpu.SMEM((n_dst * sub,), I32),
+            pltpu.SMEM((n_dst * sub,), I32),
         ],
         cost_estimate=pl.CostEstimate(flops=2 * 10 ** 10, bytes_accessed=10 ** 6, transcendentals=0),
         name='row_lists',
-    )(cnt, core, toks)
+    )(place, info)
 
 
 def rows_loop(n, fn):
@@ -194,17 +207,14 @@
     return 0.5 * v * (1.0 + jnp.tanh(math.sqrt(2.0 / math.pi) * (v + 0.044715 * v * v * v)))
 
 
-def expert_kernel(k, first, *refs):
-    if first:
-        (src, dst, cs, core_ref, x_hbm, wa_own, wa_sib, wb_own, wb_sib, send,
-         xbuf, obuf, wa, wb, t_e, t_base, t_cnt, gsem, ssem, wsem) = refs
-    else:
-        (src, dst, cs, core_ref, x_hbm, wa_own, wa_sib, wb_own, wb_sib, _, send,
-         xbuf, obuf, wa, wb, t_e, t_base, t_cnt, gsem, ssem, wsem) = refs
+def expert_kernel(k, n_chunk, first, *refs):
+    (src, seg_start, seg_len, seg_dst, cs, place, x_hbm, wa_own, wa_sib, wb_own, wb_sib) = refs[:11]
+    (send, xbuf, obuf, wa, wb, t_e, t_base, t_cnt, gsem, ssem, wsem) = refs[11 if first else 12:]
     e_loc, d_model, _ = wa_own.shape
     sub = 2 * e_loc
-    core = core_ref[0]
+    core = place[0]
     sublanes = d_model // LANES
+    n_dst = seg_start.shape[0] // (sub * n_chunk)
 
     def weight_copies(e, act):
         slot = e % 2
@@ -223,8 +233,8 @@
     weight_copies(0, lambda c: c.start())
 
     def plan(e, t):
-        lo = cs[e, k]
-        n = cs[e, k + 1] - lo
+        lo = cs[e * (n_chunk + 1) + k]
+        n = cs[e * (n_chunk + 1) + k + 1] - lo
 
         def put(i, c):
             t_e[t + i] = e
@@ -239,18 +249,34 @@
     n_all = lax.fori_loop(0, sub, plan, 0)
 
     def gather_start(t):
-        e, base, slot = t_e[t], t_base[t], t % 2
+        base, slot = t_base[t], t % 2
         rows_loop(t_cnt[t], lambda r: pltpu.make_async_copy(
-            x_hbm.at[src[e, base + r]], xbuf.at[slot, r], gsem.at[slot]).start())
+            x_hbm.at[src[base + r]], xbuf.at[slot, r], gsem.at[slot]).start())
 
     def gather_wait(t):
         n, slot = t_cnt[t], t % 2
         pltpu.make_async_copy(x_hbm.at[pl.ds(0, n)], xbuf.at[slot, pl.ds(0, n)], gsem.at[slot]).wait()
 
     def scatter_start(t):
-        e, base, slot = t_e[t], t_base[t], t % 2
-        rows_loop(t_cnt[t], lambda r: pltpu.make_async_copy(
-            obuf.at[slot, r], send.at[dst[e, base + r]], ssem.at[slot]).start())
+        base, slot = t_base[t], t % 2
+        end = base + t_cnt[t]
+
+        def segment(i, c):
+            j = (t_e[t] * n_chunk + k) * n_dst + i
+            first_row = seg_start[j]
+            lo = jnp.maximum(first_row, base)
+            n = jnp.minimum(first_row + seg_len[j], end) - lo
+
+            @pl.when(n > 0)
+            def _():
+                pltpu.make_async_copy(
+                    obuf.at[slot, pl.ds(lo - base, n)],
+                    send.at[pl.ds(seg_dst[j] + lo - first_row, n)],
+                    ssem.at[slot],
+                ).start()
+            return c
+
+        lax.fori_loop(0, n_dst, segment, 0)
 
     def scatter_wait(t):
         n, slot = t_cnt[t], t % 2
@@ -269,7 +295,7 @@
             weight_copies(e + 1, lambda c: c.start())
 
         ws = e % 2
-        n = cs[e, k + 1] - cs[e, k]
+        n = cs[e * (n_chunk + 1) + k + 1] - cs[e * (n_chunk + 1) + k]
 
         def one_tile(i, t):
             slot = t % 2
@@ -300,18 +326,18 @@
             scatter_wait(n_all - back)
 
 
-def run_experts(k, src, dst, cs, core, x_rows, wa, wa_sib, wb, wb_sib, send, send_rows):
+def run_experts(k, n_chunk, lists, place, x_rows, wa, wa_sib, wb, wb_sib, send, send_rows):
     e_loc, d_model, ff = wa.shape
     sub = 2 * e_loc
     sublanes = d_model // LANES
     first = send is None
-    ops = (src, dst, cs, core, x_rows, wa, wa_sib, wb, wb_sib) + (() if first else (send,))
-    max_tiles = sub * (pl.cdiv(src.shape[1], TILE) + 1)
+    ops = (*lists, place, x_rows, wa, wa_sib, wb, wb_sib) + (() if first else (send,))
+    max_tiles = sub * (pl.cdiv(lists[0].shape[0] // sub, TILE) + 1)
     flops = 4 * d_model * ff * x_rows.shape[0]
     return pl.pallas_call(
-        functools.partial(expert_kernel, k, first),
+        functools.partial(expert_kernel, k, n_chunk, first),
         out_shape=jax.ShapeDtypeStruct((send_rows, sublanes, LANES), BF16),
-        in_specs=[SMEM] * 4 + [HBM] * (len(ops) - 4),
+        in_specs=[SMEM] * 6 + [HBM] * (len(ops) - 6),
         out_specs=HBM,
         scratch_shapes=[
             pltpu.VMEM((2, TILE, sublanes, LANES), BF16),
@@ -332,34 +358,54 @@
     )(*ops)
 
 
-def return_kernel(rows_main, rows_last, n_y, n_x, send, recv, ssem, rsem):
+def flows_of(n_y, n_x):
+    wrap = lambda d, n: d - n if 2 * d > n else d
+    direct, relayed = [], []
+    for dy in range(n_y):
+        for dx in range(n_x):
+            if (dy, dx) == (0, 0):
+                continue
+            tie_y, tie_x = n_y >= 4 and 2 * dy == n_y, n_x >= 4 and 2 * dx == n_x
+            if not (tie_y or tie_x):
+                direct.append((dy, dx))
+                continue
+            sy, sx = wrap(dy, n_y), wrap(dx, n_x)
+            if tie_y and tie_x:
+                leg = (sy // 2, sx // 2)
+            elif tie_x:
+                sx = sx if dy % 2 == 0 else -sx
+                leg = (0, sx // 2)
+            else:
+                sy = sy if dx % 2 == 0 else -sy
+                leg = (sy // 2, 0)
+            relayed.append(((dy, dx), leg, (sy - leg[0], sx - leg[1])))
+    direct.sort(key=lambda o: -abs(wrap(o[0], n_y)) - abs(wrap(o[1], n_x)))
+    return direct, relayed
+
+
+def return_kernel(rows_main, rows_last, n_y, n_x, send, recv, stage, dsem, lsem, fsem):
     y = lax.axis_index('ep2')
     ec = lax.axis_index('ep')
     x, core = ec // 2, ec % 2
-    me = y * n_x + x
-    offsets = [(dy, dx) for dy in range(n_y) for dx in range(n_x) if (dy, dx) != (0, 0)]
-    half_y, half_x = n_y // 2, n_x // 2
-    near = lambda d, n: min(d, n - d)
-    offsets.sort(key=lambda o: (near(o[0], n_y) + near(o[1], n_x), o[0] > half_y, o[1] > half_x))
+    direct, relayed = flows_of(n_y, n_x)
+
+    def at(dy, dx):
+        return lax.rem(y + dy + n_y, n_y), lax.rem(x + dx + n_x, n_x)
+
+    def chip(dy, dx):
+        ty, tx = at(dy, dx)
+        return ty * n_x + tx
 
     def peer(dy, dx):
-        return {'ep2': lax.rem(y + dy, n_y), 'ep': lax.rem(x + dx, n_x) * 2 + core}
+        ty, tx = at(dy, dx)
+        return {'ep2': ty, 'ep': tx * 2 + core}
 
     barrier = pltpu.get_barrier_semaphore()
-    for dy, dx in offsets:
-        pl.semaphore_signal(barrier, inc=1, device_id=peer(dy, dx), device_id_type=pl.DeviceIdType.MESH)
-    pl.semaphore_wait(barrier, len(offsets))
-
-    def copy(i, dy, dx, rows):
-        ty, tx = lax.rem(y + dy, n_y), lax.rem(x + dx, n_x)
-        return pltpu.make_async_remote_copy(
-            src_ref=send.at[ty * n_x + tx, pl.ds(0, rows)],
-            dst_ref=recv.at[me, pl.ds(0, rows)],
-            send_sem=ssem.at[i],
-            recv_sem=rsem.at[i],
-            device_id=peer(dy, dx),
-            device_id_type=pl.DeviceIdType.MESH,
-        )
+    for dy in range(n_y):
+        for dx in range(n_x):
+            if (dy, dx) != (0, 0):
+                pl.semaphore_signal(barrier, inc=1, device_id=peer(dy, dx), device_id_type=pl.DeviceIdType.MESH)
+    pl.semaphore_wait(barrier, n_y * n_x - 1)
 
     def sized(row, fn):
         if rows_main == rows_last:
@@ -374,33 +420,79 @@
         def _():
             fn(rows_last)
 
-    for i, (dy, dx) in enumerate(offsets):
-        sized(lax.rem(y + dy, n_y), lambda rows: copy(i, dy, dx, rows).start())
-    for i, (dy, dx) in enumerate(offsets):
-        sized(lax.rem(y + dy, n_y), lambda rows: copy(i, dy, dx, rows).wait_send())
-    for i, (dy, dx) in enumerate(offsets):
-        sized(y, lambda rows: copy(i, dy, dx, rows).wait_recv())
+    def part(p, rows):
+        return pl.ds(p * (rows // 2), rows // 2)
+
+    def remote(src, dst, sems, i, to):
+        return pltpu.make_async_remote_copy(
+            src_ref=src, dst_ref=dst, send_sem=sems.at[0, i], recv_sem=sems.at[1, i],
+            device_id=peer(*to), device_id_type=pl.DeviceIdType.MESH)
+
+    def straight(i, rows):
+        d = direct[i]
+        return remote(send.at[chip(*d), pl.ds(0, rows)], recv.at[chip(0, 0), pl.ds(0, rows)], dsem, i, d)
+
+    def lead(i, p, rows):
+        d, leg, _ = relayed[i]
+        return remote(send.at[chip(*d), part(p, rows)], stage.at[i, part(p, rows)], lsem, 2 * i + p, leg)
+
+    def follow(i, p, rows):
+        _, leg, rest = relayed[i]
+        return remote(stage.at[i, part(p, rows)], recv.at[chip(-leg[0], -leg[1]), part(p, rows)], fsem, 2 * i + p, rest)
+
+    pieces = [(i, p) for p in range(2) for i in range(len(relayed))]
+    for i, p in pieces:
+        sized(at(*relayed[i][0])[0], lambda rows: lead(i, p, rows).start())
+    for i, d in enumerate(direct):
+        sized(at(*d)[0], lambda rows: straight(i, rows).start())
+    for i, p in pieces:
+        def forward(rows):
+            lead(i, p, rows).wait_recv()
+            follow(i, p, rows).start()
+        sized(at(*relayed[i][2])[0], forward)
+    for i, p in pieces:
+        sized(at(*relayed[i][0])[0], lambda rows: lead(i, p, rows).wait_send())
+    for i, d in enumerate(direct):
+        sized(at(*d)[0], lambda rows: straight(i, rows).wait_send())
+    for i, p in pieces:
+        sized(at(*relayed[i][2])[0], lambda rows: follow(i, p, rows).wait_send())
+
+    def arrivals(rows):
+        for i in range(len(direct)):
+            straight(i, rows).wait_recv()
+        for i, p in pieces:
+            follow(i, p, rows).wait_recv()
+
+    sized(y, arrivals)
 
 
 def send_back(rows_main, rows_last, cid, n_y, n_x, send):
-    n = n_y * n_x - 1
+    direct, relayed = flows_of(n_y, n_x)
+    n_d, n_r = len(direct), max(1, len(relayed))
     return pl.pallas_call(
         functools.partial(return_kernel, rows_main, rows_last, n_y, n_x),
-        out_shape=jax.ShapeDtypeStruct(send.shape, BF16),
+        out_shape=(
+            jax.ShapeDtypeStruct(send.shape, BF16),
+            jax.ShapeDtypeStruct((n_r, *send.shape[1:]), BF16),
+        ),
         in_specs=[HBM],
-        out_specs=HBM,
-        scratch_shapes=[pltpu.SemaphoreType.DMA((n,)), pltpu.SemaphoreType.DMA((n,))],
+        out_specs=(HBM, HBM),
+        scratch_shapes=[
+            pltpu.SemaphoreType.DMA((2, n_d)),
+            pltpu.SemaphoreType.DMA((2, 2 * n_r)),
+            pltpu.SemaphoreType.DMA((2, 2 * n_r)),
+        ],
         compiler_params=pltpu.CompilerParams(collective_id=cid, has_side_effects=True),
         name='send_back_%d_%d' % (rows_main, rows_last),
-    )(send)
-
-
-def combine_kernel(tok, wgt, kept, chip_ref, recv, send, x_ref, y_ref, rbuf, acc0, acc1, acc2, acc3, sem):
+    )(send)[0]
+
+
+def combine_kernel(tok, wgt, kept, place, recv, send, x_ref, y_ref, rbuf, acc0, acc1, acc2, acc3, sem):
     n_tok, d_model = x_ref.shape
     n_chip, slots, sublanes, _ = recv.shape
     sub = kept.shape[0] // n_chip
     accs = (acc0, acc1, acc2, acc3)
-    mine = chip_ref[0]
+    mine = place[1]
     blk = 16
 
     def count(i):
@@ -440,16 +532,16 @@
         fetch(i, lambda d: d.wait())
 
         def one_expert(q, base):
-            e = i * sub + q
-            n = kept[e]
+            first = (i * sub + q) * LANES
+            n = kept[i * sub + q]
 
             def quad(b, cc):
+                at = first + b * 4
+                toks = [tok[at + p] for p in range(4)]
+                wgts = [wgt[at + p] for p in range(4)]
+                rows = [wgts[p] * rbuf[slot, base + b * 4 + p].astype(F32) for p in range(4)]
                 for p in range(4):
-                    s = b * 4 + p
-                    s_in = jnp.minimum(s, LANES - 1)
-                    t = jnp.where(s < n, tok[e, s_in], n_tok)
-                    row = rbuf[slot, base + s].astype(F32)
-                    accs[p][t] = accs[p][t] + wgt[e, s_in] * row
+                    accs[p][toks[p]] = accs[p][toks[p]] + rows[p]
                 return cc
 
             lax.fori_loop(0, (n + 3) // 4, quad, 0)
@@ -469,7 +561,7 @@
     lax.fori_loop(0, n_tok // blk, finish, 0)
 
 
-def combine(tok, wgt, kept, chip, recv, send, x):
+def combine(tok, wgt, kept, place, recv, send, x):
     n_tok, d_model = x.shape
     n_chip, slots, sublanes, _ = recv.shape
     acc = pltpu.VMEM((n_tok + 8, sublanes, LANES), F32)
@@ -486,7 +578,7 @@
         compiler_params=pltpu.CompilerParams(vmem_limit_bytes=VMEM_LIMIT),
         cost_estimate=pl.CostEstimate(flops=2 * 10 ** 10, bytes_accessed=6 * 10 ** 7, transcendentals=0),
         name='combine',
-    )(tok, wgt, kept, chip, recv, send, x)
+    )(tok, wgt, kept, place, recv, send, x)
 
 
 def solution(mesh):
@@ -505,28 +597,27 @@
         cap = capacity_of(group, n_tok, n_top, experts)
         sublanes = d_model // LANES
         slots = sub * LANES
-        step = n_tok // CHUNKS
+        bounds = tuple(n_tok * q // CHUNK_UNITS for q in CHUNK_ENDS)
+        n_chunk = len(bounds) - 1
         me = lax.axis_index(dev_axes)
         core, chip = me % 2, me // 2
+        place = jnp.stack([core, chip]).astype(I32)
 
         x3 = x_loc.reshape(n_tok, sublanes, LANES)
-        chunks = [lax.all_gather(x3[k * step:(k + 1) * step], dev_axes, tiled=True) for k in range(CHUNKS)]
+        chunks = [lax.all_gather(x3[bounds[k]:bounds[k + 1]], dev_axes, tiled=True) for k in range(n_chunk)]
         swap = [(i, i ^ 1) for i in range(n_ep)]
         w_a_sib = lax.ppermute(w_a, 'ep', swap)
         w_b_sib = lax.ppermute(w_b, 'ep', swap)
 
-        toks, wgts, cnts = route(ids_loc, gate_loc)
-        info = jnp.concatenate([toks[:experts].reshape(n_chip, sub, LANES), jnp.pad(cnts, ((0, sub - PREFIX_ROWS), (0, 0)))[None]], axis=0)
-        info, chunks[0] = lax.optimization_barrier((info, chunks[0]))
-        every = lax.all_gather(info, dev_axes, tiled=False)
-        cnt_all = every[:, n_chip, :CHUNKS + 1, :]
-        my_cnt = lax.dynamic_slice(cnt_all, (0, 0, chip * sub), (group, CHUNKS + 1, sub)).reshape(-1)
-        by_core = every.reshape(n_chip, 2, n_chip + 1, sub, LANES)
-        my_tok = lax.dynamic_slice(by_core, (0, core, chip, 0, 0), (n_chip, 1, 1, sub, LANES)).reshape(n_chip * sub, LANES)
-        core1 = core.reshape(1).astype(I32)
-        src, dst, cs = build_lists(my_cnt, core1, my_tok, cap, slots, n_tok, group, sub)
-
-        totals = cnt_all[:, CHUNKS, :experts]
+        toks, wgts, cnts = route(ids_loc, gate_loc, bounds)
+        for_chip = toks[:experts].reshape(n_chip, 1, sub, LANES)
+        table = jnp.concatenate([
+            jnp.broadcast_to(for_chip, (n_chip, 2, sub, LANES)).reshape(group, sub, LANES),
+            jnp.broadcast_to(cnts[None], (group, PREFIX_ROWS, LANES))], axis=1)
+        table = lax.all_to_all(table, dev_axes, 0, 0, tiled=True)
+        lists = build_lists(place, table.reshape(-1), cap, slots, bounds, group, sub)
+
+        totals = table[:, sub + n_chunk, :experts]
         offs = jnp.cumsum(totals, axis=0) - totals
         kept = jnp.clip(cap - offs, 0, totals)
         kept_own = lax.dynamic_slice(kept, (me, 0), (1, experts)).reshape(experts)
@@ -535,8 +626,8 @@
         need_last = jnp.max(need[n_y - 1])
 
         send = None
-        for k in range(CHUNKS):
-            send = run_experts(k, src, dst, cs, core1, chunks[k], w_a, w_a_sib, w_b, w_b_sib, send, n_chip * slots)
+        for k in range(n_chunk):
+            send = run_experts(k, n_chunk, lists, place, chunks[k], w_a, w_a_sib, w_b, w_b_sib, send, n_chip * slots)
         send = send.reshape(n_chip, slots, sublanes, LANES)
 
         tiers = [(slots * a // 64, slots * b // 64) for a, b in ((43, 32), (45, 36), (49, 36), (53, 40))] + [(slots, slots)]
@@ -545,7 +636,9 @@
             fits = jnp.logical_and(need_main <= tiers[i][0], need_last <= tiers[i][1])
             index = jnp.where(fits, jnp.int32(i), index)
         recv = lax.switch(index, [functools.partial(send_back, a, b, i, n_y, n_x) for i, (a, b) in enumerate(tiers)], send)
-        return combine(toks, wgts, kept_own, chip.reshape(1).astype(I32), recv, send, x_loc)
+        lane = jnp.arange(LANES)
+        put_at = jnp.where(lane[None, :] < kept_own[:, None], toks[:experts], n_tok).reshape(-1)
+        return combine(put_at, wgts[:experts].reshape(-1), kept_own, place, recv, send, x_loc)
 
     tok_spec = P(('dp', 'ep2', 'ep'), None)
     w_spec = P(dev_axes, None, None)

time: 1440 us -> 1230 us (0.85)
  Pallas kernels: 1190 us -> 967 us
    pallas_call x1, Pallas kernels: 835 us -> 695 us  [send_back(): pl.pallas_call(functools.partial(return_kernel, rows_main, rows_last, n_y...]
    pallas_call x6 -> x5, Pallas kernels: 291 us -> 233 us  [the longest x3 166 us: run_experts(): pl.pallas_call(functools.partial(expert_kernel, k, n_chunk, first), out_s...]
    pallas_call x1, Pallas kernels: 59.9 us -> 39.4 us  [combine(): pl.pallas_call(combine_kernel, out_shape=jax.ShapeDtypeStruct((n_tok, d_m...]
    all_gather x5 -> x3, waiting for transfers between devices: 214 us -> 195 us  [local_step(): lax.all_gather(x3[bounds[k]:bounds[k + 1]], dev_axes, tiled=True)]
  transfers between devices with their start and end apart: 7 -> 6, of which waited for: 4 -> 4; matrix products, arithmetic and copies ran while one was open for 1% -> 1% of each run, Pallas kernels for 17% -> 15%
where the time goes in v2:
time: 1230 us; the launch traced here: 1220 us
  Pallas kernels  967 us (79%)
  waiting for transfers between devices  205 us (17%)
  between operations  17.6 us (1%)
  local copies, waits for them, and re-layouts  13.8 us (1%)
    pallas_call x1, Pallas kernels, send_back(): pl.pallas_call(functools.partial(return_kernel, rows_main, rows_last, n_y...  695 us
    all_gather x3, waiting for transfers between devices, local_step(): lax.all_gather(x3[bounds[k]:bounds[k + 1]], dev_axes, tiled=True)  195 us
    pallas_call x3, Pallas kernels, run_experts(): pl.pallas_call(functools.partial(expert_kernel, k, n_chunk, first), out_s...  166 us
    pallas_call x1, Pallas kernels, combine(): pl.pallas_call(combine_kernel, out_shape=jax.ShapeDtypeStruct((n_tok, d_m...  39.4 us
    pallas_call x1, Pallas kernels, build_lists(): pl.pallas_call(functools.partial(list_kernel, cap, slots, bounds, group,...  38.3 us
    pallas_call x1, Pallas kernels, route(): pl.pallas_call(functools.partial(route_kernel, bounds), out_shape=(jax.Sh...  28.4 us
  transfers between devices with their start and end apart: 6, of which 4 were waited for; matrix products, arithmetic and copies ran while one was open for 1% of the time, Pallas kernels for 15%

profile of v2, /device:TPU:107, one launch (start us, length us, event | category | flops | bytes accessed | tf_op | source)
XLA Modules:
  0.0 1216.8 jit_solution(658009867389362971)
XLA Ops:
  6.5 0.0 all-gather.8.cloned.1.call-start
  6.6 1.7 slice_bitcast_fusion.1
  8.2 1.2 copy.24
  9.4 0.1 all-gather.8.cloned.1.call-update
  9.5 0.1 all-gather.6.cloned.1.call-start
  9.6 1.7 slice_bitcast_fusion
  11.3 2.0 copy.23
  13.3 0.1 all-gather.6.cloned.1.call-update
  13.3 0.1 all-gather.4.cloned.1.call-start
  13.4 1.3 copy.22
  14.7 0.1 all-gather.4.cloned.1.call-update
  14.7 0.7 collective-permute-start
  15.4 0.1 collective-permute-start.1
  15.6 1.8 copy.18.ids_ref
  17.4 1.8 copy.19.gate_ref
  19.1 28.4 %route.1 = (s32[128,128]{1,0:T(8,128)}, f32[128,128]{1,0:T(8,128)}, s32[8,128]{1,0:T(8,128)}) custom-call(s32[1024,8]{1,0:T(8,128)} %copy.18.ids_ref, f32[1024,8]{1,0:T(8,128)} %copy.19.gate_ref), custom_call_target="tpu_custom_call" | custom-call | flops 20000000000 | bytes 1000000 | tf_op jit(solution)/shard_map/route/pallas_call | solution.py:78
  47.5 0.8 broadcast_in_dim.19
  48.4 0.7 broadcast_in_dim.20
  49.1 0.7 pad_add_fusion
  49.8 7.4 all-to-all-start
  57.3 0.7 pad_add_fusion.1.place_ref.refs_5_.place
  57.9 9.3 all-to-all-done
  67.2 0.0 copy-start
  67.2 0.1 reduce_window_sum.13
  67.3 0.2 reduce_window_sum.14
  67.4 0.2 squeeze.7
  67.6 0.6 minimum_reduce_fusion
  68.2 0.7 slice_reduce_fusion
  70.1 0.7 slice_reduce_fusion.1
  73.9 0.0 copy-start.1
  73.9 0.5 copy-done.1
  74.5 1.5 select_bitcast_fusion.tok
  76.0 0.0 copy-done
  76.0 38.3 %row_lists.1 = (s32[16448]{0:T(1024)}, s32[384]{0:T(512)}, s32[384]{0:T(512)}, s32[384]{0:T(512)}, s32[32]{0:T(128)}) custom-call(s32[2]{0:T(128)} %pad_add_fusion.1.place_ref.refs_5_.place, s32[65536]{0:T(1024)} %bitcast.29), custom_call_target="tpu_custom_call" | custom-call | flops 20000000000 | bytes 1000000 | tf_op jit(solution)/shard_map/row_lists/pallas_call | solution.py:171
  114.3 0.0 collective-permute-done.refs_8_
  114.3 0.0 collective-permute-done.1.refs_10_
  114.3 7.3 all-gather.8.cloned.1.call-done.refs_6_
  121.6 47.7 %experts.3.refs_11_ = bf16[16384,16,128]{2,1,0:T(8,128)(2,1)} custom-call(s32[16448]{0:T(1024)} %get-tuple-element.32.refs_0_, s32[384]{0:T(512)} %get-tuple-element.33.refs_1_, s32[384]{0:T(512)} %get-tuple-element.34.refs_2_, s32[384]{0:T(512)} %get-tuple-element.35.refs_3_, s32[32]{0:T(128)} %get-tuple-element.36.refs_4_, ...), custom_call_target="tpu_custom_call" | custom-call | flops 51539607552 | bytes 60000000 | tf_op jit(solution)/shard_map/experts/pallas_call | solution.py:337
  169.2 149.4 %all-gather.6.cloned.1.call-done.refs_6_ = bf16[16384,16,128]{2,1,0:T(8,128)(2,1)} async-done(((bf16[512,16,128]{2,1,0:T(8,128)(2,1)}), bf16[16384,16,128]{2,1,0:T(8,128)(2,1)}) %all-gather.6.cloned.1.call-update) | async-done | bytes 67108880 | tf_op jit(solution)/shard_map/all_gather | solution.py:607
  318.6 71.0 %experts.4.refs_11_ = bf16[16384,16,128]{2,1,0:T(8,128)(2,1)} custom-call(s32[16448]{0:T(1024)} %get-tuple-element.32.refs_0_, s32[384]{0:T(512)} %get-tuple-element.33.refs_1_, s32[384]{0:T(512)} %get-tuple-element.34.refs_2_, s32[384]{0:T(512)} %get-tuple-element.35.refs_3_, s32[32]{0:T(128)} %get-tuple-element.36.refs_4_, ...), custom_call_target="tpu_custom_call", output_to_operand_aliasing={{}: (11, {})} | custom-call | flops 103079215104 | bytes 60000000 | tf_op jit(solution)/shard_map/experts/pallas_call | solution.py:337
  389.6 38.7 %all-gather.4.cloned.1.call-done.refs_6_ = bf16[8192,16,128]{2,1,0:T(8,128)(2,1)} async-done(((bf16[256,16,128]{2,1,0:T(8,128)(2,1)}), bf16[8192,16,128]{2,1,0:T(8,128)(2,1)}) %all-gather.4.cloned.1.call-update) | async-done | bytes 33554448 | tf_op jit(solution)/shard_map/all_gather | solution.py:607
  428.3 47.6 %experts.5 = bf16[16384,16,128]{2,1,0:T(8,128)(2,1)} custom-call(s32[16448]{0:T(1024)} %get-tuple-element.32.refs_0_, s32[384]{0:T(512)} %get-tuple-element.33.refs_1_, s32[384]{0:T(512)} %get-tuple-element.34.refs_2_, s32[384]{0:T(512)} %get-tuple-element.35.refs_3_, s32[32]{0:T(128)} %get-tuple-element.36.refs_4_, ...), custom_call_target="tpu_custom_call", output_to_operand_aliasing={{}: (11, {})} | custom-call | flops 51539607552 | bytes 60000000 | tf_op jit(solution)/shard_map/experts/pallas_call | solution.py:337
  475.9 694.9 %conditional.1 = (bf16[16,1024,16,128]{3,2,1,0:T(8,128)(2,1)}) conditional(s32[]{:T(128)} %clamp.3, bf16[16,1024,16,128]{3,2,1,0:T(8,128)(2,1)} %bitcast.9.send, bf16[16,1024,16,128]{3,2,1,0:T(8,128)(2,1)} %bitcast.9.send, bf16[16,1024,16,128]{3,2,1,0:T(8,128)(2,1)} %bitcast.9.send, ...), branch_computations={%region_4.5_spmd, %region_5.6_spmd, %region_6.7_spmd, %region_7.8_... | conditional | bytes 8 | solution.py:638
  476.0 694.9 %send_back_784_576.1 = (bf16[16,1024,16,128]{3,2,1,0:T(8,128)(2,1)}, bf16[7,1024,16,128]{3,2,1,0:T(8,128)(2,1)}) custom-call(bf16[16,1024,16,128]{3,2,1,0:T(8,128)(2,1)} %send.2), custom_call_target="tpu_custom_call" | custom-call | tf_op jit(solution)/shard_map/cond/branch_2_fun/send_back_784_576/pallas_call | solution.py:472
  1170.8 39.4 %combine.1 = bf16[1024,2048]{1,0:T(8,128)(2,1)} custom-call(s32[16384]{0:T(1024)} %select_bitcast_fusion.tok, f32[16384]{0:T(1024)} %bitcast.34, s32[128]{0:T(128)} %copy-done.1, s32[2]{0:T(128)} %pad_add_fusion.1.place_ref.refs_5_.place, bf16[16,1024,16,128]{3,2,1,0:T(8,128)(2,1)} %get-tuple-element.39.recv, bf16[16,1024,16,128]{3,2,1,0:T(8,128)(2,1)} %bitcast.9.send, ...), custom_call_target="tpu_custom_call" | custom-call | flops 20000000000 | bytes 60000000 | tf_op jit(solution)/shard_map/combine/pallas_call | solution.py:568
  (2 shorter events, 0.0 us)
Async XLA Ops:
  6.5 115.0 %all-gather.8.cloned.1.call-start = ((), (), s32[]{:S(2)}) async-start(), calls=%async_computation.3 | async-start | bytes 34603008 | tf_op jit(solution)/shard_map/all_gather | solution.py:607
  9.5 309.1 %all-gather.6.cloned.1.call-start = ((), (), s32[]{:S(2)}) async-start(), calls=%async_computation.2 | async-start | bytes 69206016 | tf_op jit(solution)/shard_map/all_gather | solution.py:607
  13.3 415.0 %all-gather.4.cloned.1.call-start = ((), (), s32[]{:S(2)}) async-start(), calls=%async_computation.1 | async-start | bytes 34603008 | tf_op jit(solution)/shard_map/all_gather | solution.py:607
  14.7 99.6 %collective-permute-start = (bf16[4,2048,768]{2,1,0:T(8,128)(2,1)}, bf16[4,2048,768]{2,1,0:T(8,128)(2,1)}, u32[]{:S(2)}, u32[]{:S(2)}) collective-permute-start(bf16[4,2048,768]{2,1,0:T(8,128)(2,1)} %refs_7_.5), channel_id=1, source_target_pairs={{0,1},{1,0},{2,3},{3,2},{4,5},{5,4},{6,7},{7,6},{8,9},{9,8},{10,11... | collective-permute-start | bytes 37748744 | tf_op jit(solution)/shard_map/ppermute | solution.py:609
  15.4 98.9 %collective-permute-start.1 = (bf16[4,768,2048]{2,1,0:T(8,128)(2,1)}, bf16[4,768,2048]{2,1,0:T(8,128)(2,1)}, u32[]{:S(2)}, u32[]{:S(2)}) collective-permute-start(bf16[4,768,2048]{2,1,0:T(8,128)(2,1)} %refs_9_.5), channel_id=1, source_target_pairs={{0,1},{1,0},{2,3},{3,2},{4,5},{5,4},{6,7},{7,6},{8,9},{9,8},{10,11... | collective-permute-start | bytes 37748744 | tf_op jit(solution)/shard_map/ppermute | solution.py:610
  49.8 17.4 %all-to-all-start = ((s32[32,16,128]{2,1,0:T(8,128)}), s32[32,16,128]{2,1,0:T(8,128)S(1)}, u32[]{:S(2)}, u32[]{:S(2)}) async-start(s32[32,16,128]{2,1,0:T(8,128)} %pad_add_fusion), calls=%async_computation | async-start | bytes 524288 | tf_op jit(solution)/shard_map/all_to_all | solution.py:617
  67.2 8.8 copy-start
  73.9 0.5 copy-start.1
Sparse Core Ops, SparseCore 0:
  9.6 111.9 all-gather.7
  123.7 194.8 all-gather.5
  320.7 107.5 all-gather.3

commit v3 on v2

v3 whole, which is shorter than its diff:
```python
import functools
import math

import jax
import jax.numpy as jnp
from jax import lax
from jax.experimental import pallas as pl
from jax.experimental.pallas import tpu as pltpu
from jax.sharding import PartitionSpec as P

LANES = 128
CHUNK_UNITS = 16
CHUNK_ENDS = (0, 4, 12, 16)
SIZES = (40, 42, 44, 46, 48, 52, 64)
TILE = 256
PREFIX_ROWS = 8
BF16 = jnp.bfloat16
F32 = jnp.float32
I32 = jnp.int32
HBM = pl.BlockSpec(memory_space=pl.ANY)
SMEM = pl.BlockSpec(memory_space=pltpu.SMEM)
VMEM = pl.BlockSpec(memory_space=pltpu.VMEM)
VMEM_LIMIT = 64_000_000


def capacity_of(group_size, n_tok, n_top, experts):
    return 8 * ((5 * group_size * n_tok * n_top) // (32 * experts))


def route_kernel(bounds, ids_ref, gate_ref, tok_ref, wgt_ref, cnt_ref, code_t, gate_t, tok_acc, wgt_acc):
    n_tok, n_top = ids_ref.shape
    lane = lax.broadcasted_iota(I32, (n_tok, LANES), 1)
    member = jnp.zeros((n_tok, LANES), F32)
    gates = jnp.zeros((n_tok, LANES), F32)
    for j in range(n_top):
        hit = ids_ref[:, j:j + 1] == lane
        member = member + jnp.where(hit, 1.0, 0.0)
        gates = gates + jnp.where(hit, gate_ref[:, j:j + 1], 0.0)
    member_b = member.astype(BF16)
    row_block = min(n_tok, 128)
    for i in range(n_tok // row_block):
        rows = pl.ds(i * row_block, row_block)
        later = lax.broadcasted_iota(I32, (row_block, n_tok), 0) + i * row_block
        earlier = lax.broadcasted_iota(I32, (row_block, n_tok), 1)
        tri = jnp.where(earlier < later, 1.0, 0.0).astype(BF16)
        rank = jnp.dot(tri, member_b, preferred_element_type=F32)
        mem = member[i * row_block:(i + 1) * row_block]
        code_t[:, rows] = jnp.where(mem > 0.5, rank, -1.0).T
        gate_t[:, rows] = gates[i * row_block:(i + 1) * row_block].T
    total = jnp.zeros((1, LANES), F32)
    rows_out = [total]
    for lo, hi in zip(bounds[:-1], bounds[1:]):
        total = total + jnp.sum(member[lo:hi], axis=0, keepdims=True)
        rows_out.append(total)
    while len(rows_out) < PREFIX_ROWS:
        rows_out.append(total)
    cnt_ref[...] = jnp.concatenate(rows_out, axis=0).astype(I32)
    tok_acc[...] = jnp.zeros_like(tok_acc)
    wgt_acc[...] = jnp.zeros_like(wgt_acc)
    slot = lax.broadcasted_iota(I32, (LANES, n_tok), 0).astype(F32)
    token = lax.broadcasted_iota(I32, (1, n_tok), 1).astype(F32)
    out_lane = lax.broadcasted_iota(I32, (LANES, LANES), 1)

    def one_expert(e, carry):
        hit = slot == code_t[pl.ds(e, 1), :]
        tok = jnp.sum(jnp.where(hit, token, 0.0), axis=1, keepdims=True)
        wgt = jnp.sum(jnp.where(hit, gate_t[pl.ds(e, 1), :], 0.0), axis=1, keepdims=True)
        tok_acc[...] = jnp.where(out_lane == e, tok, tok_acc[...])
        wgt_acc[...] = jnp.where(out_lane == e, wgt, wgt_acc[...])
        return carry

    lax.fori_loop(0, LANES, one_expert, 0)
    tok_ref[...] = tok_acc[...].T.astype(I32)
    wgt_ref[...] = wgt_acc[...].T


def route(ids, gate, bounds):
    n_tok = ids.shape[0]
    return pl.pallas_call(
        functools.partial(route_kernel, bounds),
        out_shape=(
            jax.ShapeDtypeStruct((LANES, LANES), I32),
            jax.ShapeDtypeStruct((LANES, LANES), F32),
            jax.ShapeDtypeStruct((PREFIX_ROWS, LANES), I32),
        ),
        in_specs=[VMEM, VMEM],
        out_specs=(VMEM, VMEM, VMEM),
        scratch_shapes=[
            pltpu.VMEM((LANES, n_tok), F32),
            pltpu.VMEM((LANES, n_tok), F32),
            pltpu.VMEM((LANES, LANES), F32),
            pltpu.VMEM((LANES, LANES), F32),
        ],
        cost_estimate=pl.CostEstimate(flops=2 * 10 ** 10, bytes_accessed=10 ** 6, transcendentals=0),
        name='route',
    )(ids, gate)


def list_kernel(cap, slots_a, slots_b, bounds, n_y, n_x, sub, place_ref, info_ref, src_ref, start_ref, len_ref, dst_a_ref, dst_b_ref, cs_ref,
                kept_ref, base_a_ref, base_b_ref):
    core, chip = place_ref[0], place_ref[1]
    n_dst = n_y * n_x
    n_chunk = len(bounds) - 1
    dev_words = (sub + PREFIX_ROWS) * LANES
    width = src_ref.shape[0] // sub

    def count(g, k, e):
        return info_ref[g * dev_words + (sub + k) * LANES + chip * sub + e]

    def per_expert(e, carry):
        def per_dev(i, off):
            for c in range(2):
                n = count(2 * i + c, n_chunk, e)
                kept = jnp.clip(cap - off, 0, n)
                off = off + n

                @pl.when(core == c)
                def _():
                    kept_ref[i * sub + e] = kept
            return off
        lax.fori_loop(0, n_dst, per_dev, 0)
        return carry

    lax.fori_loop(0, sub, per_expert, 0)

    def add_up(base_ref, i, acc):
        def add(e, acc):
            base_ref[i * sub + e] = acc
            return acc + kept_ref[i * sub + e]
        return lax.fori_loop(0, sub, add, acc)

    for x in range(n_x):
        lax.fori_loop(0, n_y, lambda y, acc: add_up(base_a_ref, y * n_x + x, acc), x * slots_a)
    for y in range(n_y):
        lax.fori_loop(0, n_x, lambda x, acc: add_up(base_b_ref, y * n_x + x, acc), y * slots_b)

    def expert_lists(e, carry):
        pos = e * width
        for k in range(n_chunk):
            cs_ref[e * (n_chunk + 1) + k] = pos
            size = bounds[k + 1] - bounds[k]

            def segment(i, o):
                g = 2 * i + core
                kept = kept_ref[i * sub + e]
                s0 = jnp.minimum(count(g, k, e), kept)
                n = jnp.minimum(count(g, k + 1, e), kept) - s0
                j = (e * n_chunk + k) * n_dst + i
                start_ref[j] = o
                len_ref[j] = n
                dst_a_ref[j] = base_a_ref[i * sub + e] + s0
                dst_b_ref[j] = base_b_ref[i * sub + e] + s0
                src0 = g * size - bounds[k]
                tok0 = g * dev_words + e * LANES + s0

                def block(b, c):
                    vals = [info_ref[tok0 + b * 8 + q] for q in range(8)]
                    for q in range(8):
                        src_ref[o + b * 8 + q] = src0 + vals[q]
                    return c

                lax.fori_loop(0, (n + 7) // 8, block, 0)
                return o + n

            pos = lax.fori_loop(0, n_dst, segment, pos)
        cs_ref[e * (n_chunk + 1) + n_chunk] = pos
        return carry

    lax.fori_loop(0, sub, expert_lists, 0)


def build_lists(place, info, cap, slots_a, slots_b, bounds, n_y, n_x, sub):
    n_dst, n_chunk = n_y * n_x, len(bounds) - 1
    width = LANES * n_dst + 8
    segs = sub * n_chunk * n_dst
    return pl.pallas_call(
        functools.partial(list_kernel, cap, slots_a, slots_b, bounds, n_y, n_x, sub),
        out_shape=(
            jax.ShapeDtypeStruct((sub * width,), I32),
            jax.ShapeDtypeStruct((segs,), I32),
            jax.ShapeDtypeStruct((segs,), I32),
            jax.ShapeDtypeStruct((segs,), I32),
            jax.ShapeDtypeStruct((segs,), I32),
            jax.ShapeDtypeStruct((sub * (n_chunk + 1),), I32),
        ),
        in_specs=[SMEM, SMEM],
        out_specs=(SMEM,) * 6,
        scratch_shapes=[
            pltpu.SMEM((n_dst * sub,), I32),
            pltpu.SMEM((n_dst * sub,), I32),
            pltpu.SMEM((n_dst * sub,), I32),
        ],
        cost_estimate=pl.CostEstimate(flops=2 * 10 ** 10, bytes_accessed=10 ** 6, transcendentals=0),
        name='row_lists',
    )(place, info)


def rows_loop(n, fn):
    def block(b, c):
        for q in range(8):
            fn(b * 8 + q)
        return c

    def single(r, c):
        fn(r)
        return c

    full = n // 8
    lax.fori_loop(0, full, block, 0)
    lax.fori_loop(full * 8, n, single, 0)


def gelu(v):
    return 0.5 * v * (1.0 + jnp.tanh(math.sqrt(2.0 / math.pi) * (v + 0.044715 * v * v * v)))


def expert_kernel(k, n_chunk, first, *refs):
    (src, seg_start, seg_len, seg_dst_a, seg_dst_b, cs, place, x_hbm, wa_own, wa_sib, wb_own, wb_sib) = refs[:12]
    (send_a, send_b, xbuf, obuf_a, obuf_b, wa, wb, t_e, t_base, t_cnt, gsem, ssem, wsem) = refs[12 if first else 14:]
    e_loc, d_model, _ = wa_own.shape
    sub = 2 * e_loc
    core = place[0]
    sublanes = d_model // LANES
    n_dst = seg_start.shape[0] // (sub * n_chunk)

    def weight_copies(e, act):
        slot = e % 2
        q = e % e_loc

        @pl.when(e // e_loc == core)
        def _():
            act(pltpu.make_async_copy(wa_own.at[q], wa.at[slot], wsem.at[slot, 0]))
            act(pltpu.make_async_copy(wb_own.at[q], wb.at[slot], wsem.at[slot, 1]))

        @pl.when(e // e_loc != core)
        def _():
            act(pltpu.make_async_copy(wa_sib.at[q], wa.at[slot], wsem.at[slot, 0]))
            act(pltpu.make_async_copy(wb_sib.at[q], wb.at[slot], wsem.at[slot, 1]))

    sides = ((obuf_a, send_a, seg_dst_a), (obuf_b, send_b, seg_dst_b))
    weight_copies(0, lambda c: c.start())

    def plan(e, t):
        lo = cs[e * (n_chunk + 1) + k]
        n = cs[e * (n_chunk + 1) + k + 1] - lo

        def put(i, c):
            t_e[t + i] = e
            t_base[t + i] = lo + i * TILE
            t_cnt[t + i] = jnp.minimum(n - i * TILE, TILE)
            return c

        n_tiles = (n + TILE - 1) // TILE
        lax.fori_loop(0, n_tiles, put, 0)
        return t + n_tiles

    n_all = lax.fori_loop(0, sub, plan, 0)

    def gather_start(t):
        base, slot = t_base[t], t % 2
        rows_loop(t_cnt[t], lambda r: pltpu.make_async_copy(
            x_hbm.at[src[base + r]], xbuf.at[slot, r], gsem.at[slot]).start())

    def gather_wait(t):
        n, slot = t_cnt[t], t % 2
        pltpu.make_async_copy(x_hbm.at[pl.ds(0, n)], xbuf.at[slot, pl.ds(0, n)], gsem.at[slot]).wait()

    def scatter_start(t):
        base, slot = t_base[t], t % 2
        end = base + t_cnt[t]

        def segment(i, c):
            j = (t_e[t] * n_chunk + k) * n_dst + i
            first_row = seg_start[j]
            lo = jnp.maximum(first_row, base)
            n = jnp.minimum(first_row + seg_len[j], end) - lo

            @pl.when(n > 0)
            def _():
                for half, (obuf, send, seg_dst) in enumerate(sides):
                    pltpu.make_async_copy(
                        obuf.at[slot, pl.ds(lo - base, n)],
                        send.at[pl.ds(seg_dst[j] + lo - first_row, n)],
                        ssem.at[half, slot],
                    ).start()
            return c

        lax.fori_loop(0, n_dst, segment, 0)

    def scatter_wait(t):
        n, slot = t_cnt[t], t % 2
        for half, (obuf, send, _) in enumerate(sides):
            pltpu.make_async_copy(obuf.at[slot, pl.ds(0, n)], send.at[pl.ds(0, n)], ssem.at[half, slot]).wait()

    for t in range(2):
        @pl.when(t < n_all)
        def _():
            gather_start(t)

    def one_expert(e, t_first):
        weight_copies(e, lambda c: c.wait())

        @pl.when(e + 1 < sub)
        def _():
            weight_copies(e + 1, lambda c: c.start())

        ws = e % 2
        n = cs[e * (n_chunk + 1) + k + 1] - cs[e * (n_chunk + 1) + k]

        def one_tile(i, t):
            slot = t % 2
            gather_wait(t)

            @pl.when(t >= 2)
            def _():
                scatter_wait(t - 2)

            rows = xbuf[slot].reshape(TILE, d_model)
            hidden = gelu(jnp.dot(rows, wa[ws], preferred_element_type=F32)).astype(BF16)
            out = jnp.dot(hidden, wb[ws], preferred_element_type=F32).astype(BF16)
            obuf_a[slot] = out[:, :d_model // 2].reshape(TILE, sublanes // 2, LANES)
            obuf_b[slot] = out[:, d_model // 2:].reshape(TILE, sublanes // 2, LANES)

            @pl.when(t + 2 < n_all)
            def _():
                gather_start(t + 2)

            scatter_start(t)
            return t + 1

        return lax.fori_loop(0, (n + TILE - 1) // TILE, one_tile, t_first)

    lax.fori_loop(0, sub, one_expert, 0)
    for back in (2, 1):
        @pl.when(n_all >= back)
        def _():
            scatter_wait(n_all - back)


def run_experts(k, n_chunk, lists, place, x_rows, wa, wa_sib, wb, wb_sib, sends, rows_a, rows_b):
    e_loc, d_model, ff = wa.shape
    sub = 2 * e_loc
    sublanes = d_model // LANES
    half = sublanes // 2
    first = sends is None
    ops = (*lists, place, x_rows, wa, wa_sib, wb, wb_sib) + (() if first else tuple(sends))
    n_smem = len(lists) + 1
    max_tiles = sub * (pl.cdiv(lists[0].shape[0] // sub, TILE) + 1)
    flops = 4 * d_model * ff * x_rows.shape[0]
    return pl.pallas_call(
        functools.partial(expert_kernel, k, n_chunk, first),
        out_shape=(
            jax.ShapeDtypeStruct((rows_a, half, LANES), BF16),
            jax.ShapeDtypeStruct((rows_b, half, LANES), BF16),
        ),
        in_specs=[SMEM] * n_smem + [HBM] * (len(ops) - n_smem),
        out_specs=(HBM, HBM),
        scratch_shapes=[
            pltpu.VMEM((2, TILE, sublanes, LANES), BF16),
            pltpu.VMEM((2, TILE, half, LANES), BF16),
            pltpu.VMEM((2, TILE, half, LANES), BF16),
            pltpu.VMEM((2, d_model, ff), BF16),
            pltpu.VMEM((2, ff, d_model), BF16),
            pltpu.SMEM((max_tiles,), I32),
            pltpu.SMEM((max_tiles,), I32),
            pltpu.SMEM((max_tiles,), I32),
            pltpu.SemaphoreType.DMA((2,)),
            pltpu.SemaphoreType.DMA((2, 2)),
            pltpu.SemaphoreType.DMA((2, 2)),
        ],
        input_output_aliases={} if first else {len(ops) - 2: 0, len(ops) - 1: 1},
        compiler_params=pltpu.CompilerParams(vmem_limit_bytes=VMEM_LIMIT),
        cost_estimate=pl.CostEstimate(flops=flops, bytes_accessed=6 * 10 ** 7, transcendentals=0),
        name='experts',
    )(*ops)


PIECES = 4


class Ring:
    def __init__(self, axis, n_y, n_x):
        y, ec = lax.axis_index('ep2'), lax.axis_index('ep')
        self.axis, self.core = axis, ec % 2
        self.n = n_x if axis == 'x' else n_y
        self.pos = ec // 2 if axis == 'x' else y
        far = self.n // 2 if self.n % 2 == 0 and self.n >= 4 else None
        self.direct = [d for d in range(1, self.n) if d != far]
        self.far = far

    def place(self, d):
        return lax.rem(self.pos + d + self.n, self.n)

    def device(self, d):
        if self.axis == 'x':
            return {'ep': self.place(d) * 2 + self.core}
        return {'ep2': self.place(d)}

    def remote(self, src, dst, sems, i, d):
        return pltpu.make_async_remote_copy(
            src_ref=src, dst_ref=dst, send_sem=sems.at[0, i], recv_sem=sems.at[1, i],
            device_id=self.device(d), device_id_type=pl.DeviceIdType.MESH)

    def signal(self, barrier):
        for d in range(1, self.n):
            pl.semaphore_signal(barrier, inc=1, device_id=self.device(d), device_id_type=pl.DeviceIdType.MESH)


def spread_kernel(rows_a, rows_b, n_y, n_x, send_a, send_b, recv_a, recv_b, stage_a, stage_b, sem_a, sem_b):
    rings = (Ring('x', n_y, n_x), Ring('y', n_y, n_x))
    barrier = pltpu.get_barrier_semaphore()
    for ring in rings:
        ring.signal(barrier)
    pl.semaphore_wait(barrier, n_x + n_y - 2)

    sides = list(zip(rings, (rows_a, rows_b), (send_a, send_b), (recv_a, recv_b), (stage_a, stage_b), (sem_a, sem_b)))

    def lead(side, p):
        ring, rows, send, _, stage, sem = side
        hop = ring.far // 2 if p % 2 == 0 else -(ring.far // 2)
        part = pl.ds(p * (rows // PIECES), rows // PIECES)
        return ring.remote(send.at[ring.place(ring.far), part], stage.at[part], sem, p, hop)

    def follow(side, p):
        ring, rows, _, recv, stage, sem = side
        hop = ring.far // 2 if p % 2 == 0 else -(ring.far // 2)
        part = pl.ds(p * (rows // PIECES), rows // PIECES)
        return ring.remote(stage.at[part], recv.at[ring.place(-hop), part], sem, PIECES + p, hop)

    def straight(side, i):
        ring, rows, send, recv, _, sem = side
        d = ring.direct[i]
        return ring.remote(send.at[ring.place(d), pl.ds(0, rows)], recv.at[ring.pos, pl.ds(0, rows)], sem, 2 * PIECES + i, d)

    relayed = [(side, p) for p in range(PIECES) for side in sides if side[0].far]
    direct = [(side, i) for side in sides for i in range(len(side[0].direct))]
    for job in relayed:
        lead(*job).start()
    for job in direct:
        straight(*job).start()
    for job in relayed:
        lead(*job).wait_recv()
        follow(*job).start()
    for job in relayed:
        lead(*job).wait_send()
    for job in direct:
        straight(*job).wait()
    for job in relayed:
        follow(*job).wait()


def spread(rows_a, rows_b, cid, n_y, n_x, send_a, send_b):
    return pl.pallas_call(
        functools.partial(spread_kernel, rows_a, rows_b, n_y, n_x),
        out_shape=tuple(jax.ShapeDtypeStruct(s, BF16) for s in (send_a.shape, send_b.shape, send_a.shape[1:], send_b.shape[1:])),
        in_specs=[HBM, HBM],
        out_specs=(HBM,) * 4,
        scratch_shapes=[
            pltpu.SemaphoreType.DMA((2, 2 * PIECES + n_x)),
            pltpu.SemaphoreType.DMA((2, 2 * PIECES + n_y)),
        ],
        compiler_params=pltpu.CompilerParams(collective_id=cid, has_side_effects=True),
        name='spread_%d_%d' % (rows_a, rows_b),
    )(send_a, send_b)[:2]


def sum_kernel(n_y, n_x, kept_a, kept_b, place, tok_hbm, wgt_hbm, recv_a, recv_b, send_a, send_b, z_a, z_b,
               tok, wgt, rbuf, acc0, acc1, tsem, rsem, zsem):
    core, chip = place[0], place[1]
    my_y, my_x = chip // n_x, chip % n_x
    n_chip = n_y * n_x
    sub = kept_a.shape[0] // n_chip
    n_tok = z_a.shape[1]
    words = sub * LANES
    per_dev = tok_hbm.shape[0] // (2 * n_chip)
    blk = 16
    accs = (acc0, acc1)

    def tables(half, act):
        for i in range(n_y if half == 0 else n_x):
            g = (i * n_x + my_x) * 2 + core if half == 0 else (my_y * n_x + i) * 2 + core
            for q in range(n_x if half == 0 else n_y):
                owner = my_y * n_x + q if half == 0 else q * n_x + my_x
                src = pl.ds(pl.multiple_of(g * per_dev + owner * words, words), words)
                dst = pl.ds((half * n_chip + i * (n_x if half == 0 else n_y) + q) * words, words)
                act(pltpu.make_async_copy(tok_hbm.at[src], tok.at[dst], tsem.at[half]))
                act(pltpu.make_async_copy(wgt_hbm.at[src], wgt.at[dst], tsem.at[half]))

    for half in range(2):
        tables(half, lambda c: c.start())

    def one_half(half, kept, recv, send, z, mine, n_dst, n_src):
        def count(q):
            def add(i, n):
                for e in range(sub):
                    n = n + kept[(i * n_src + q) * sub + e]
                return n
            return lax.fori_loop(0, n_dst, add, 0)

        def fetch(q, act):
            slot, n = q % 2, count(q)

            @pl.when(jnp.logical_and(q == mine, n > 0))
            def _():
                act(pltpu.make_async_copy(send.at[q, pl.ds(0, n)], rbuf.at[slot, pl.ds(0, n)], rsem.at[slot]))

            @pl.when(jnp.logical_and(q != mine, n > 0))
            def _():
                act(pltpu.make_async_copy(recv.at[q, pl.ds(0, n)], rbuf.at[slot, pl.ds(0, n)], rsem.at[slot]))

        fetch(0, lambda c: c.start())

        def zero(b, c):
            for acc in accs:
                acc[pl.ds(b * blk, blk)] = jnp.zeros((blk, *acc.shape[1:]), F32)
            return c

        lax.fori_loop(0, n_dst * n_tok // blk, zero, 0)
        tables(half, lambda c: c.wait())
        dummy = n_dst * n_tok

        def one_source(q, c):
            slot = q % 2

            @pl.when(q + 1 < n_src)
            def _():
                fetch(q + 1, lambda d: d.start())

            fetch(q, lambda d: d.wait())

            def one_list(j, base):
                i, e = j // sub, j % sub
                n = kept[(i * n_src + q) * sub + e]
                first = (half * n_chip + i * n_src + q) * words + e * LANES
                shift = i * n_tok

                def quad(b, cc):
                    at = first + b * 4
                    toks = [jnp.where(b * 4 + p < n, shift + tok[at + p], dummy) for p in range(4)]
                    wgts = [wgt[at + p] for p in range(4)]
                    rows = [wgts[p] * rbuf[slot, base + b * 4 + p].astype(F32) for p in range(4)]
                    for p in range(4):
                        acc = accs[p % 2]
                        acc[toks[p]] = acc[toks[p]] + rows[p]
                    return cc

                lax.fori_loop(0, (n + 3) // 4, quad, 0)
                return base + n

            lax.fori_loop(0, n_dst * sub, one_list, 0)
            return c

        lax.fori_loop(0, n_src, one_source, 0)

        def put(i):
            return pltpu.make_async_copy(acc0.at[pl.ds(i * n_tok, n_tok)], z.at[i], zsem.at[i])

        for i in range(n_dst):
            def merge(b, c):
                rows = pl.ds(i * n_tok + b * blk, blk)
                acc0[rows] = acc0[rows] + acc1[rows]
                return c
            lax.fori_loop(0, n_tok // blk, merge, 0)
            put(i).start()
        for i in range(n_dst):
            put(i).wait()

    one_half(0, kept_a, recv_a, send_a, z_a, my_x, n_y, n_x)
    one_half(1, kept_b, recv_b, send_b, z_b, my_y, n_x, n_y)


def weighted_sums(n_y, n_x, kept_a, kept_b, place, tok, wgt, recv_a, recv_b, send_a, send_b, n_tok):
    half = recv_a.shape[2]
    n_dst = max(n_y, n_x)
    slots = max(recv_a.shape[1], recv_b.shape[1])
    words = kept_a.shape[0] * LANES
    acc = pltpu.VMEM((n_dst * n_tok + 8, half, LANES), F32)
    return pl.pallas_call(
        functools.partial(sum_kernel, n_y, n_x),
        out_shape=(
            jax.ShapeDtypeStruct((n_y, n_tok, half, LANES), F32),
            jax.ShapeDtypeStruct((n_x, n_tok, half, LANES), F32),
        ),
        in_specs=[SMEM] * 3 + [HBM] * 6,
        out_specs=(HBM, HBM),
        scratch_shapes=[
            pltpu.SMEM((2 * words,), I32),
            pltpu.SMEM((2 * words,), F32),
            pltpu.VMEM((2, slots + 8, half, LANES), BF16),
            acc, acc,
            pltpu.SemaphoreType.DMA((2,)),
            pltpu.SemaphoreType.DMA((2,)),
            pltpu.SemaphoreType.DMA((n_dst,)),
        ],
        compiler_params=pltpu.CompilerParams(vmem_limit_bytes=VMEM_LIMIT),
        cost_estimate=pl.CostEstimate(flops=2 * 10 ** 10, bytes_accessed=6 * 10 ** 7, transcendentals=0),
        name='weighted_sums',
    )(kept_a, kept_b, place, tok, wgt, recv_a, recv_b, send_a, send_b)


SUM_CHUNKS = 4


def reduce_kernel(n_y, n_x, z_a, z_b, x_ref, y_ref, own, part, zsem, rsem):
    rings = (Ring('y', n_y, n_x), Ring('x', n_y, n_x))
    zs = (z_a, z_b)
    n_tok, d_model = x_ref.shape
    rows = n_tok // (2 * SUM_CHUNKS)
    half = d_model // 2
    blk = 16
    lanes = [(a, w) for a in range(2) for w in range(2)]
    steps = [ring.n - 1 for ring in rings]

    barrier = pltpu.get_barrier_semaphore()
    for ring in rings:
        for d in (1, -1):
            pl.semaphore_signal(barrier, inc=1, device_id=ring.device(d), device_id_type=pl.DeviceIdType.MESH)
    pl.semaphore_wait(barrier, 4)

    def sign(w):
        return 1 if w == 0 else -1

    def chunk(w, j):
        return pl.ds((w * SUM_CHUNKS + j) * rows, rows)

    def load(a, w, s, j):
        block = rings[a].place(-sign(w) * (s + 1)) if s < steps[a] else rings[a].pos
        return pltpu.make_async_copy(zs[a].at[block, chunk(w, j)], own.at[a, w, s - 1, j], zsem.at[a, w, s - 1, j])

    def hop(a, w, s, j):
        ring = rings[a]
        src = zs[a].at[ring.place(-sign(w)), chunk(w, j)] if s == 0 else part.at[a, w, s - 1, j]
        return pltpu.make_async_remote_copy(
            src_ref=src, dst_ref=part.at[a, w, s, j], send_sem=rsem.at[0, a, w, s, j], recv_sem=rsem.at[1, a, w, s, j],
            device_id=ring.device(sign(w)), device_id_type=pl.DeviceIdType.MESH)

    for j in range(SUM_CHUNKS):
        for a, w in lanes:
            hop(a, w, 0, j).start()
    for s in range(1, max(steps) + 1):
        for j in range(SUM_CHUNKS):
            for a, w in lanes:
                if s <= steps[a]:
                    load(a, w, s, j).start()

    for s in range(1, max(steps)):
        for j in range(SUM_CHUNKS):
            for a, w in lanes:
                if s >= steps[a]:
                    continue
                load(a, w, s, j).wait()
                hop(a, w, s - 1, j).wait_recv()

                def add(b, c):
                    r = pl.ds(b * blk, blk)
                    part[a, w, s - 1, j, r] = part[a, w, s - 1, j, r] + own[a, w, s - 1, j, r]
                    return c

                lax.fori_loop(0, rows // blk, add, 0)
                hop(a, w, s, j).start()

    for j in range(SUM_CHUNKS):
        for a, w in lanes:
            s = steps[a]
            load(a, w, s, j).wait()
            hop(a, w, s - 1, j).wait_recv()
            first = (w * SUM_CHUNKS + j) * rows

            def finish(b, c):
                r = pl.ds(b * blk, blk)
                out = pl.ds(pl.multiple_of(first + b * blk, blk), blk)
                cols = pl.ds(a * half, half)
                total = part[a, w, s - 1, j, r] + own[a, w, s - 1, j, r]
                y_ref[out, cols] = (x_ref[out, cols].astype(F32) + total.reshape(blk, half)).astype(BF16)
                return c

            lax.fori_loop(0, rows // blk, finish, 0)
    for s in range(max(steps)):
        for j in range(SUM_CHUNKS):
            for a, w in lanes:
                if s < steps[a]:
                    hop(a, w, s, j).wait_send()


def reduce_back(cid, n_y, n_x, z_a, z_b, x):
    n_tok, d_model = x.shape
    rows = n_tok // (2 * SUM_CHUNKS)
    steps = max(n_y, n_x) - 1
    buf = pltpu.VMEM((2, 2, steps, SUM_CHUNKS, rows, z_a.shape[2], LANES), F32)
    return pl.pallas_call(
        functools.partial(reduce_kernel, n_y, n_x),
        out_shape=jax.ShapeDtypeStruct((n_tok, d_model), BF16),
        in_specs=[HBM, HBM, VMEM],
        out_specs=VMEM,
        scratch_shapes=[
            buf, buf,
            pltpu.SemaphoreType.DMA((2, 2, steps, SUM_CHUNKS)),
            pltpu.SemaphoreType.DMA((2, 2, 2, steps, SUM_CHUNKS)),
        ],
        compiler_params=pltpu.CompilerParams(collective_id=cid, has_side_effects=True, vmem_limit_bytes=VMEM_LIMIT),
        name='reduce_back',
    )(z_a, z_b, x)


def solution(mesh):
    dev_axes = ('ep2', 'ep')
    n_y, n_ep = mesh.shape['ep2'], mesh.shape['ep']
    n_x = n_ep // 2
    group = n_y * n_ep
    n_chip = n_y * n_x

    def local_step(x_loc, ids_loc, gate_loc, w_a, w_b):
        n_tok, d_model = x_loc.shape
        n_top = ids_loc.shape[1]
        e_loc = w_a.shape[0]
        sub = 2 * e_loc
        experts = e_loc * group
        cap = capacity_of(group, n_tok, n_top, experts)
        sublanes = d_model // LANES
        slots_a, slots_b = n_y * sub * LANES, n_x * sub * LANES
        bounds = tuple(n_tok * q // CHUNK_UNITS for q in CHUNK_ENDS)
        n_chunk = len(bounds) - 1
        me = lax.axis_index(dev_axes)
        core, chip = me % 2, me // 2
        place = jnp.stack([core, chip]).astype(I32)

        x3 = x_loc.reshape(n_tok, sublanes, LANES)
        chunks = [lax.all_gather(x3[bounds[k]:bounds[k + 1]], dev_axes, tiled=True) for k in range(n_chunk)]
        swap = [(i, i ^ 1) for i in range(n_ep)]
        w_a_sib = lax.ppermute(w_a, 'ep', swap)
        w_b_sib = lax.ppermute(w_b, 'ep', swap)

        toks, wgts, cnts = route(ids_loc, gate_loc, bounds)
        for_chip = toks[:experts].reshape(n_chip, 1, sub, LANES)
        table = jnp.concatenate([
            jnp.broadcast_to(for_chip, (n_chip, 2, sub, LANES)).reshape(group, sub, LANES),
            jnp.broadcast_to(cnts[None], (group, PREFIX_ROWS, LANES))], axis=1)
        table = lax.all_to_all(table, dev_axes, 0, 0, tiled=True)
        lists = build_lists(place, table.reshape(-1), cap, slots_a, slots_b, bounds, n_y, n_x, sub)

        totals = table[:, sub + n_chunk, :experts]
        offs = jnp.cumsum(totals, axis=0) - totals
        kept = jnp.clip(cap - offs, 0, totals)
        by_place = kept.reshape(n_y, n_x, 2, n_y, n_x, sub)
        y, x = chip // n_x, chip % n_x
        kept_a = lax.dynamic_slice(by_place, (0, x, core, y, 0, 0), (n_y, 1, 1, 1, n_x, sub)).reshape(-1)
        kept_b = lax.dynamic_slice(by_place, (y, 0, core, 0, x, 0), (1, n_x, 1, n_y, 1, sub)).reshape(-1)
        per_chip = jnp.sum(by_place, axis=5)
        need_a = jnp.max(jnp.sum(per_chip, axis=0))
        need_b = jnp.max(jnp.sum(per_chip, axis=1))

        sends = None
        for k in range(n_chunk):
            if k == n_chunk - 1:
                toks, wgts, sends = lax.optimization_barrier((toks, wgts, sends))
            sends = run_experts(k, n_chunk, lists, place, chunks[k], w_a, w_a_sib, w_b, w_b_sib, sends, n_x * slots_a, n_y * slots_b)
        tok_all = lax.all_gather(toks[:experts].reshape(-1), dev_axes, tiled=True)
        wgt_all = lax.all_gather(wgts[:experts].reshape(-1), dev_axes, tiled=True)
        send_a = sends[0].reshape(n_x, slots_a, sublanes // 2, LANES)
        send_b = sends[1].reshape(n_y, slots_b, sublanes // 2, LANES)

        tiers = [(slots_a * q // 64, slots_b * q // 64) for q in SIZES]
        index = jnp.int32(len(tiers) - 1)
        for i in range(len(tiers) - 2, -1, -1):
            fits = jnp.logical_and(need_a <= tiers[i][0], need_b <= tiers[i][1])
            index = jnp.where(fits, jnp.int32(i), index)
        recv_a, recv_b = lax.switch(index, [functools.partial(spread, a, b, i, n_y, n_x) for i, (a, b) in enumerate(tiers)], send_a, send_b)
        recv_a, tok_all, wgt_all = lax.optimization_barrier((recv_a, tok_all, wgt_all))
        z_a, z_b = weighted_sums(n_y, n_x, kept_a, kept_b, place, tok_all, wgt_all, recv_a, recv_b, send_a, send_b, n_tok)
        return reduce_back(len(tiers), n_y, n_x, z_a, z_b, x_loc)

    tok_spec = P(('dp', 'ep2', 'ep'), None)
    w_spec = P(dev_axes, None, None)
    return jax.shard_map(local_step, mesh=mesh, in_specs=(tok_spec, tok_spec, tok_spec, w_spec, w_spec), out_specs=tok_spec, check_vma=False)
```

time: 1230 us -> 1000 us (0.81)
  Pallas kernels: 967 us -> 714 us
  waiting for transfers between devices: 205 us -> 218 us
    pallas_call x3 -> x4, Pallas kernels: 773 us -> 540 us  [the longest x1 262 us: spread(): pl.pallas_call(functools.partial(spread_kernel, rows_a, rows_b, n_y, n_x)...]
    pallas_call x3, Pallas kernels: 166 us -> 145 us  [run_experts(): pl.pallas_call(functools.partial(expert_kernel, k, n_chunk, first), out_s...]
    all_gather x3, waiting for transfers between devices: 195 us -> 208 us  [local_step(): lax.all_gather(x3[bounds[k]:bounds[k + 1]], dev_axes, tiled=True)]
  transfers between devices with their start and end apart: 6 -> 8, of which waited for: 4 -> 4; matrix products, arithmetic and copies ran while one was open for 1% -> 2% of each run, Pallas kernels for 15% -> 48%
where the time goes in v3:
time: 1000 us; the launch traced here: 985 us
  Pallas kernels  714 us (71%)
  waiting for transfers between devices  218 us (22%)
  between operations  21 us (2%)
  local copies, waits for them, and re-layouts  19.9 us (2%)
    pallas_call x1, Pallas kernels, spread(): pl.pallas_call(functools.partial(spread_kernel, rows_a, rows_b, n_y, n_x)...  262 us
    all_gather x3, waiting for transfers between devices, local_step(): lax.all_gather(x3[bounds[k]:bounds[k + 1]], dev_axes, tiled=True)  208 us
    pallas_call x3, Pallas kernels, run_experts(): pl.pallas_call(functools.partial(expert_kernel, k, n_chunk, first), out_s...  145 us
    pallas_call x1, Pallas kernels, reduce_back(): pl.pallas_call(functools.partial(reduce_kernel, n_y, n_x), out_shape=jax....  143 us
    pallas_call x1, Pallas kernels, weighted_sums(): pl.pallas_call(functools.partial(sum_kernel, n_y, n_x), out_shape=(jax.Sh...  98.5 us
    pallas_call x1, Pallas kernels, build_lists(): pl.pallas_call(functools.partial(list_kernel, cap, slots_a, slots_b, boun...  36.7 us
    pallas_call x1, Pallas kernels, route(): pl.pallas_call(functools.partial(route_kernel, bounds), out_shape=(jax.Sh...  28.4 us
  transfers between devices with their start and end apart: 8, of which 4 were waited for; matrix products, arithmetic and copies ran while one was open for 2% of the time, Pallas kernels for 48%

profile of v3, /device:TPU:107, one launch (start us, length us, event | category | flops | bytes accessed | tf_op | source)
XLA Modules:
  0.0 984.8 jit_solution(11168324152054873949)
XLA Ops:
  6.6 1.7 slice_bitcast_fusion.1
  8.2 1.2 copy.22
  9.5 0.1 all-gather.10.cloned.1.call-update
  9.5 0.1 all-gather.8.cloned.1.call-start
  9.6 1.7 slice_bitcast_fusion
  11.3 2.0 copy.21
  13.3 0.1 all-gather.8.cloned.1.call-update
  13.4 0.1 all-gather.6.cloned.1.call-start
  13.4 1.3 copy.20
  14.7 0.1 all-gather.6.cloned.1.call-update
  14.8 0.7 collective-permute-start
  15.5 0.1 collective-permute-start.1
  15.6 1.0 copy.18.ids_ref
  16.6 1.0 copy.19.gate_ref
  17.6 28.4 %route.1 = (s32[128,128]{1,0:T(8,128)}, f32[128,128]{1,0:T(8,128)}, s32[8,128]{1,0:T(8,128)}) custom-call(s32[1024,8]{1,0:T(8,128)} %copy.18.ids_ref, f32[1024,8]{1,0:T(8,128)} %copy.19.gate_ref), custom_call_target="tpu_custom_call" | custom-call | flops 20000000000 | bytes 1000000 | tf_op jit(solution)/shard_map/route/pallas_call | solution.py:79
  46.0 0.8 broadcast_in_dim.14
  46.9 0.7 broadcast_in_dim.15
  47.6 0.7 pad_add_fusion
  48.3 7.4 all-to-all-start
  55.7 0.1 all-gather.12.cloned.1.call-start
  55.8 0.6 pad_add_fusion.1.place_ref.refs_6_.place
  56.5 9.2 all-to-all-done
  65.6 0.7 copy-done
  66.4 36.7 %row_lists.1 = (s32[16448]{0:T(1024)}, s32[384]{0:T(512)}, s32[384]{0:T(512)}, s32[384]{0:T(512)}, s32[384]{0:T(512)}, /*index=5*/s32[32]{0:T(128)}) custom-call(s32[2]{0:T(128)} %pad_add_fusion.1.place_ref.refs_6_.place, s32[65536]{0:T(1024)} %bitcast.39), custom_call_target="tpu_custom_call" | custom-call | flops 20000000000 | bytes 1000000 | tf_op jit(solution)/shard_map/row_lists/pallas_call | solution.py:176
  103.1 18.5 %all-gather.10.cloned.1.call-done.refs_7_ = bf16[8192,16,128]{2,1,0:T(8,128)(2,1)} async-done(((bf16[256,16,128]{2,1,0:T(8,128)(2,1)}), bf16[8192,16,128]{2,1,0:T(8,128)(2,1)}) %all-gather.10.cloned.1.call-update) | async-done | bytes 33554448 | tf_op jit(solution)/shard_map/all_gather | solution.py:728
  121.6 41.7 %experts.3 = (bf16[16384,8,128]{2,1,0:T(8,128)(2,1)}, bf16[16384,8,128]{2,1,0:T(8,128)(2,1)}) custom-call(s32[16448]{0:T(1024)} %get-tuple-element.89.refs_0_, s32[384]{0:T(512)} %get-tuple-element.90.refs_1_, s32[384]{0:T(512)} %get-tuple-element.91.refs_2_, s32[384]{0:T(512)} %get-tuple-element.92.refs_3_, s32[384]{0:T(512)} %get-tuple-element.93.refs_4_, ...), custom_call_target="tpu_custom_call" | custom-call | flops 51539607552 | bytes 60000000 | tf_op jit(solution)/shard_map/experts/pallas_call | solution.py:350
  163.3 155.3 %all-gather.8.cloned.1.call-done.refs_7_ = bf16[16384,16,128]{2,1,0:T(8,128)(2,1)} async-done(((bf16[512,16,128]{2,1,0:T(8,128)(2,1)}), bf16[16384,16,128]{2,1,0:T(8,128)(2,1)}) %all-gather.8.cloned.1.call-update) | async-done | bytes 67108880 | tf_op jit(solution)/shard_map/all_gather | solution.py:728
  318.6 61.8 %experts.4 = (bf16[16384,8,128]{2,1,0:T(8,128)(2,1)}, bf16[16384,8,128]{2,1,0:T(8,128)(2,1)}) custom-call(s32[16448]{0:T(1024)} %get-tuple-element.89.refs_0_, s32[384]{0:T(512)} %get-tuple-element.90.refs_1_, s32[384]{0:T(512)} %get-tuple-element.91.refs_2_, s32[384]{0:T(512)} %get-tuple-element.92.refs_3_, ...), custom_call_target="tpu_custom_call", output_to_operand_aliasing={{0}: (12, {}), {1}: (13, {})} | custom-call | flops 103079215104 | bytes 60000000 | tf_op jit(solution)/shard_map/experts/pallas_call | solution.py:350
  380.4 0.1 all-gather.12.cloned.1.call-update
  380.4 0.1 all-gather.14.cloned.1.call-start
  380.6 1.0 fusion.1
  381.5 0.1 reduce_window_sum.13
  381.6 0.3 reduce_window_sum.14
  381.9 0.3 squeeze.5
  382.3 1.2 fusion
  383.5 0.6 reduce_max.18
  384.1 0.7 reduce_max.19
  392.5 0.7 reshape.44.kept_b
  393.2 0.6 reshape.43.kept_a
  393.8 0.1 all-gather.14.cloned.1.call-update
  393.9 34.4 %all-gather.6.cloned.1.call-done.refs_7_ = bf16[8192,16,128]{2,1,0:T(8,128)(2,1)} async-done(((bf16[256,16,128]{2,1,0:T(8,128)(2,1)}), bf16[8192,16,128]{2,1,0:T(8,128)(2,1)}) %all-gather.6.cloned.1.call-update) | async-done | bytes 33554448 | tf_op jit(solution)/shard_map/all_gather | solution.py:728
  428.3 41.9 %experts.5 = (bf16[16384,8,128]{2,1,0:T(8,128)(2,1)}, bf16[16384,8,128]{2,1,0:T(8,128)(2,1)}) custom-call(s32[16448]{0:T(1024)} %get-tuple-element.89.refs_0_, s32[384]{0:T(512)} %get-tuple-element.90.refs_1_, s32[384]{0:T(512)} %get-tuple-element.91.refs_2_, s32[384]{0:T(512)} %get-tuple-element.92.refs_3_, ...), custom_call_target="tpu_custom_call", output_to_operand_aliasing={{0}: (12, {}), {1}: (13, {})} | custom-call | flops 51539607552 | bytes 60000000 | tf_op jit(solution)/shard_map/experts/pallas_call | solution.py:350
  470.2 262.0 %conditional.1 = (bf16[4,4096,8,128]{3,2,1,0:T(8,128)(2,1)}, bf16[4,4096,8,128]{3,2,1,0:T(8,128)(2,1)}) conditional(s32[]{:T(128)} %clamp.3, (bf16[4,4096,8,128]{3,2,1,0:T(8,128)(2,1)}, bf16[4,4096,8,128]{3,2,1,0:T(8,128)(2,1)}) %tuple.66, (bf16[4,4096,8,128]{3,2,1,0:T(8,128)(2,1)}, ...), branch_computations={%region_5.6_spmd, %region_6.7_spmd, %region_7.8_spmd, %region_8.9_... | conditional | bytes 16 | solution.py:767
  470.2 262.0 %spread_2816_2816.1 = (bf16[4,4096,8,128]{3,2,1,0:T(8,128)(2,1)}, bf16[4,4096,8,128]{3,2,1,0:T(8,128)(2,1)}, bf16[4096,8,128]{2,1,0:T(8,128)(2,1)}, bf16[4096,8,128]{2,1,0:T(8,128)(2,1)}) custom-call(bf16[4,4096,8,128]{3,2,1,0:T(8,128)(2,1)} %get-tuple-element.41.send_a, bf16[4,4096,8,128]{3,2,1,0:T(8,128)(2,1)} %get-tuple-element.42.send_b), custom_call_target="tpu_custom_call" | custom-call | tf_op jit(solution)/shard_map/cond/branch_2_fun/spread_2816_2816/pallas_call | solution.py:453
  732.3 0.0 all-gather.12.cloned.1.call-done.tok_hbm
  732.3 98.5 %weighted_sums.1 = (f32[4,1024,8,128]{3,2,1,0:T(8,128)}, f32[4,1024,8,128]{3,2,1,0:T(8,128)}) custom-call(s32[128]{0:T(128)} %reshape.43.kept_a, s32[128]{0:T(128)} %reshape.44.kept_b, s32[2]{0:T(128)} %pad_add_fusion.1.place_ref.refs_6_.place, s32[524288]{0:T(1024)} %all-gather.12.cloned.1.call-done.tok_hbm, f32[524288]{0:T(1024)} %all-gather.14.cloned.1.call-done.wgt_hbm, ...), custom_call_target="tpu_custom_call" | custom-call | flops 20000000000 | bytes 60000000 | tf_op jit(solution)/shard_map/weighted_sums/pallas_call | solution.py:578
  830.8 142.7 %reduce_back.1 = bf16[1024,2048]{1,0:T(8,128)(2,1)} custom-call(f32[4,1024,8,128]{3,2,1,0:T(8,128)} %get-tuple-element.111.z_a, f32[4,1024,8,128]{3,2,1,0:T(8,128)} %get-tuple-element.112.z_b, bf16[1024,2048]{1,0:T(8,128)(2,1)} %x_ref.1), custom_call_target="tpu_custom_call" | custom-call | tf_op jit(solution)/shard_map/reduce_back/pallas_call | solution.py:690
  973.5 4.8 copy.42
  (11 shorter events, 0.1 us)
Async XLA Ops:
  6.5 9.1 copy-start.1
  6.5 10.1 %copy-start.2 = (f32[1024,8]{0,1:T(8,128)S(1)}, f32[1024,8]{0,1:T(8,128)}, u32[]{:S(2)}) copy-start(f32[1024,8]{0,1:T(8,128)} %param.14) | copy-start | bytes 98308
  6.6 115.0 %all-gather.10.cloned.1.call-start = ((), (), s32[]{:S(2)}) async-start(), calls=%async_computation.3 | async-start | bytes 34603008 | tf_op jit(solution)/shard_map/all_gather | solution.py:728
  9.5 309.0 %all-gather.8.cloned.1.call-start = ((), (), s32[]{:S(2)}) async-start(), calls=%async_computation.2 | async-start | bytes 69206016 | tf_op jit(solution)/shard_map/all_gather | solution.py:728
  13.4 414.9 %all-gather.6.cloned.1.call-start = ((), (), s32[]{:S(2)}) async-start(), calls=%async_computation.1 | async-start | bytes 34603008 | tf_op jit(solution)/shard_map/all_gather | solution.py:728
  14.8 88.3 %collective-permute-start = (bf16[4,2048,768]{2,1,0:T(8,128)(2,1)}, bf16[4,2048,768]{2,1,0:T(8,128)(2,1)}, u32[]{:S(2)}, u32[]{:S(2)}) collective-permute-start(bf16[4,2048,768]{2,1,0:T(8,128)(2,1)} %refs_8_.5), channel_id=1, source_target_pairs={{0,1},{1,0},{2,3},{3,2},{4,5},{5,4},{6,7},{7,6},{8,9},{9,8},{10,11... | collective-permute-start | bytes 37748744 | tf_op jit(solution)/shard_map/ppermute | solution.py:730
  15.5 87.6 %collective-permute-start.1 = (bf16[4,768,2048]{2,1,0:T(8,128)(2,1)}, bf16[4,768,2048]{2,1,0:T(8,128)(2,1)}, u32[]{:S(2)}, u32[]{:S(2)}) collective-permute-start(bf16[4,768,2048]{2,1,0:T(8,128)(2,1)} %refs_10_.5), channel_id=1, source_target_pairs={{0,1},{1,0},{2,3},{3,2},{4,5},{5,4},{6,7},{7,6},{8,9},{9,8},{10,11... | collective-permute-start | bytes 37748744 | tf_op jit(solution)/shard_map/ppermute | solution.py:731
  48.3 17.4 %all-to-all-start = ((s32[32,16,128]{2,1,0:T(8,128)}), s32[32,16,128]{2,1,0:T(8,128)S(1)}, u32[]{:S(2)}, u32[]{:S(2)}) async-start(s32[32,16,128]{2,1,0:T(8,128)} %pad_add_fusion), calls=%async_computation | async-start | bytes 524288 | tf_op jit(solution)/shard_map/all_to_all | solution.py:738
  55.7 676.6 %all-gather.12.cloned.1.call-start = ((), (), s32[]{:S(2)}) async-start(), calls=%async_computation.4 | async-start | bytes 2162688 | tf_op jit(solution)/shard_map/all_gather | solution.py:757
  65.6 0.7 copy-start
  380.4 351.9 %all-gather.14.cloned.1.call-start = ((), (), s32[]{:S(2)}) async-start(), calls=%async_computation.5 | async-start | bytes 2162688 | tf_op jit(solution)/shard_map/all_gather | solution.py:758
Sparse Core Ops, SparseCore 0:
  9.7 111.8 all-gather.9
  123.7 194.8 all-gather.7
  320.7 107.5 all-gather.5
  430.2 37.5 all-gather.11
  469.7 40.6 all-gather.13

commit v4 on v3

--- a/solution.py
+++ b/solution.py
@@ -9,8 +9,8 @@
 from jax.sharding import PartitionSpec as P
 
 LANES = 128
-CHUNK_UNITS = 16
-CHUNK_ENDS = (0, 4, 12, 16)
+CHUNK_UNITS = 32
+CHUNK_ENDS = (0, 25, 32)
 SIZES = (40, 42, 44, 46, 48, 52, 64)
 TILE = 256
 PREFIX_ROWS = 8
@@ -464,8 +464,11 @@
     )(send_a, send_b)[:2]
 
 
-def sum_kernel(n_y, n_x, kept_a, kept_b, place, tok_hbm, wgt_hbm, recv_a, recv_b, send_a, send_b, z_a, z_b,
-               tok, wgt, rbuf, acc0, acc1, tsem, rsem, zsem):
+def sum_kernel(n_y, n_x, kept_a, kept_b, place, tok_hbm, wgt_hbm, recv_a, recv_b, send_a, send_b, z_a, z_b, *scratch):
+    n_acc = 2 * max(n_y, n_x)
+    tok, wgt, rbuf = scratch[:3]
+    accs = scratch[3:3 + n_acc]
+    tsem, rsem, zsem = scratch[3 + n_acc:]
     core, chip = place[0], place[1]
     my_y, my_x = chip // n_x, chip % n_x
     n_chip = n_y * n_x
@@ -474,99 +477,111 @@
     words = sub * LANES
     per_dev = tok_hbm.shape[0] // (2 * n_chip)
     blk = 16
-    accs = (acc0, acc1)
+    halves = (
+        (kept_a, recv_a, send_a, z_a, my_x, n_y, n_x),
+        (kept_b, recv_b, send_b, z_b, my_y, n_x, n_y),
+    )
 
     def tables(half, act):
-        for i in range(n_y if half == 0 else n_x):
+        n_dst, n_src = halves[half][5:]
+        for i in range(n_dst):
             g = (i * n_x + my_x) * 2 + core if half == 0 else (my_y * n_x + i) * 2 + core
-            for q in range(n_x if half == 0 else n_y):
+            for q in range(n_src):
                 owner = my_y * n_x + q if half == 0 else q * n_x + my_x
                 src = pl.ds(pl.multiple_of(g * per_dev + owner * words, words), words)
-                dst = pl.ds((half * n_chip + i * (n_x if half == 0 else n_y) + q) * words, words)
+                dst = pl.ds((half * n_chip + i * n_src + q) * words, words)
                 act(pltpu.make_async_copy(tok_hbm.at[src], tok.at[dst], tsem.at[half]))
                 act(pltpu.make_async_copy(wgt_hbm.at[src], wgt.at[dst], tsem.at[half]))
 
+    def rows_of(half, i, q):
+        kept, n_src = halves[half][0], halves[half][6]
+        n = kept[(i * n_src + q) * sub]
+        for e in range(1, sub):
+            n = n + kept[(i * n_src + q) * sub + e]
+        return n
+
+    def fetch(half, q, act):
+        _, recv, send, _, mine, n_dst, _ = halves[half]
+        slot, n = q % 2, rows_of(half, 0, q)
+        for i in range(1, n_dst):
+            n = n + rows_of(half, i, q)
+
+        @pl.when(jnp.logical_and(q == mine, n > 0))
+        def _():
+            act(pltpu.make_async_copy(send.at[q, pl.ds(0, n)], rbuf.at[slot, pl.ds(0, n)], rsem.at[slot]))
+
+        @pl.when(jnp.logical_and(q != mine, n > 0))
+        def _():
+            act(pltpu.make_async_copy(recv.at[q, pl.ds(0, n)], rbuf.at[slot, pl.ds(0, n)], rsem.at[slot]))
+
+    def zero(acc):
+        def body(b, c):
+            acc[pl.ds(b * blk, blk)] = jnp.zeros((blk, *acc.shape[1:]), F32)
+            return c
+        lax.fori_loop(0, n_tok // blk, body, 0)
+
+    fetch(0, 0, lambda c: c.start())
     for half in range(2):
         tables(half, lambda c: c.start())
-
-    def one_half(half, kept, recv, send, z, mine, n_dst, n_src):
-        def count(q):
-            def add(i, n):
-                for e in range(sub):
-                    n = n + kept[(i * n_src + q) * sub + e]
-                return n
-            return lax.fori_loop(0, n_dst, add, 0)
-
-        def fetch(q, act):
-            slot, n = q % 2, count(q)
-
-            @pl.when(jnp.logical_and(q == mine, n > 0))
-            def _():
-                act(pltpu.make_async_copy(send.at[q, pl.ds(0, n)], rbuf.at[slot, pl.ds(0, n)], rsem.at[slot]))
-
-            @pl.when(jnp.logical_and(q != mine, n > 0))
-            def _():
-                act(pltpu.make_async_copy(recv.at[q, pl.ds(0, n)], rbuf.at[slot, pl.ds(0, n)], rsem.at[slot]))
-
-        fetch(0, lambda c: c.start())
-
-        def zero(b, c):
-            for acc in accs:
-                acc[pl.ds(b * blk, blk)] = jnp.zeros((blk, *acc.shape[1:]), F32)
-            return c
-
-        lax.fori_loop(0, n_dst * n_tok // blk, zero, 0)
+    puts = []
+    for half in range(2):
+        kept, _, _, z, _, n_dst, n_src = halves[half]
+        for i in range(n_dst):
+            zero(accs[2 * i + 1])
+        for put in puts:
+            put.wait()
+        for i in range(n_dst):
+            zero(accs[2 * i])
         tables(half, lambda c: c.wait())
-        dummy = n_dst * n_tok
-
-        def one_source(q, c):
+        for q in range(n_src):
             slot = q % 2
-
-            @pl.when(q + 1 < n_src)
-            def _():
-                fetch(q + 1, lambda d: d.start())
-
-            fetch(q, lambda d: d.wait())
-
-            def one_list(j, base):
-                i, e = j // sub, j % sub
-                n = kept[(i * n_src + q) * sub + e]
-                first = (half * n_chip + i * n_src + q) * words + e * LANES
-                shift = i * n_tok
-
-                def quad(b, cc):
-                    at = first + b * 4
-                    toks = [jnp.where(b * 4 + p < n, shift + tok[at + p], dummy) for p in range(4)]
-                    wgts = [wgt[at + p] for p in range(4)]
-                    rows = [wgts[p] * rbuf[slot, base + b * 4 + p].astype(F32) for p in range(4)]
-                    for p in range(4):
-                        acc = accs[p % 2]
-                        acc[toks[p]] = acc[toks[p]] + rows[p]
+            fetch(half, q, lambda d: d.wait())
+            if q + 1 < n_src:
+                fetch(half, q + 1, lambda d: d.start())
+            elif half == 0 and n_src % 2 == 0:
+                fetch(1, 0, lambda d: d.start())
+            bases = [jnp.int32(0)]
+            for i in range(n_dst - 1):
+                bases.append(bases[-1] + rows_of(half, i, q))
+
+            def one_expert(e, bases):
+                counts = [kept[(i * n_src + q) * sub + e] for i in range(n_dst)]
+                most = counts[0]
+                for n in counts[1:]:
+                    most = jnp.maximum(most, n)
+                firsts = [(half * n_chip + i * n_src + q) * words + e * LANES for i in range(n_dst)]
+
+                def pair(b, cc):
+                    jobs = []
+                    for i in range(n_dst):
+                        for p in range(2):
+                            s = b * 2 + p
+                            row = rbuf[slot, bases[i] + s].astype(F32)
+                            jobs.append((accs[2 * i + p], tok[firsts[i] + s], wgt[firsts[i] + s] * row))
+                    for acc, t, row in jobs:
+                        acc[t] = acc[t] + row
                     return cc
 
-                lax.fori_loop(0, (n + 3) // 4, quad, 0)
-                return base + n
-
-            lax.fori_loop(0, n_dst * sub, one_list, 0)
-            return c
-
-        lax.fori_loop(0, n_src, one_source, 0)
-
-        def put(i):
-            return pltpu.make_async_copy(acc0.at[pl.ds(i * n_tok, n_tok)], z.at[i], zsem.at[i])
-
+                lax.fori_loop(0, (most + 1) // 2, pair, 0)
+                return tuple(base + n for base, n in zip(bases, counts))
+
+            lax.fori_loop(0, sub, one_expert, tuple(bases))
+        if half == 0 and n_src % 2:
+            fetch(1, 0, lambda d: d.start())
+        puts = []
         for i in range(n_dst):
+            even, odd = accs[2 * i], accs[2 * i + 1]
+
             def merge(b, c):
-                rows = pl.ds(i * n_tok + b * blk, blk)
-                acc0[rows] = acc0[rows] + acc1[rows]
+                rows = pl.ds(b * blk, blk)
+                even[rows] = even[rows] + odd[rows]
                 return c
+
             lax.fori_loop(0, n_tok // blk, merge, 0)
-            put(i).start()
-        for i in range(n_dst):
-            put(i).wait()
-
-    one_half(0, kept_a, recv_a, send_a, z_a, my_x, n_y, n_x)
-    one_half(1, kept_b, recv_b, send_b, z_b, my_y, n_x, n_y)
+            puts.append(pltpu.make_async_copy(even.at[pl.ds(0, n_tok)], z.at[i], zsem.at[i]))
+            puts[-1].start()
+    for put in puts:
+        put.wait()
 
 
 def weighted_sums(n_y, n_x, kept_a, kept_b, place, tok, wgt, recv_a, recv_b, send_a, send_b, n_tok):
@@ -574,7 +589,6 @@
     n_dst = max(n_y, n_x)
     slots = max(recv_a.shape[1], recv_b.shape[1])
     words = kept_a.shape[0] * LANES
-    acc = pltpu.VMEM((n_dst * n_tok + 8, half, LANES), F32)
     return pl.pallas_call(
         functools.partial(sum_kernel, n_y, n_x),
         out_shape=(
@@ -586,8 +600,8 @@
         scratch_shapes=[
             pltpu.SMEM((2 * words,), I32),
             pltpu.SMEM((2 * words,), F32),
-            pltpu.VMEM((2, slots + 8, half, LANES), BF16),
-            acc, acc,
+            pltpu.VMEM((2, slots + LANES, half, LANES), BF16),
+            *[pltpu.VMEM((n_tok + 8, half, LANES), F32) for _ in range(2 * n_dst)],
             pltpu.SemaphoreType.DMA((2,)),
             pltpu.SemaphoreType.DMA((2,)),
             pltpu.SemaphoreType.DMA((n_dst,)),
@@ -741,6 +755,8 @@
         totals = table[:, sub + n_chunk, :experts]
         offs = jnp.cumsum(totals, axis=0) - totals
         kept = jnp.clip(cap - offs, 0, totals)
+        kept_own = lax.dynamic_slice(kept, (me, 0), (1, experts)).reshape(experts, 1)
+        toks = jnp.where(jnp.arange(LANES)[None, :] < kept_own, toks[:experts], n_tok)
         by_place = kept.reshape(n_y, n_x, 2, n_y, n_x, sub)
         y, x = chip // n_x, chip % n_x
         kept_a = lax.dynamic_slice(by_place, (0, x, core, y, 0, 0), (n_y, 1, 1, 1, n_x, sub)).reshape(-1)
@@ -754,7 +770,7 @@
             if k == n_chunk - 1:
                 toks, wgts, sends = lax.optimization_barrier((toks, wgts, sends))
             sends = run_experts(k, n_chunk, lists, place, chunks[k], w_a, w_a_sib, w_b, w_b_sib, sends, n_x * slots_a, n_y * slots_b)
-        tok_all = lax.all_gather(toks[:experts].reshape(-1), dev_axes, tiled=True)
+        tok_all = lax.all_gather(toks.reshape(-1), dev_axes, tiled=True)
         wgt_all = lax.all_gather(wgts[:experts].reshape(-1), dev_axes, tiled=True)
         send_a = sends[0].reshape(n_x, slots_a, sublanes // 2, LANES)
         send_b = sends[1].reshape(n_y, slots_b, sublanes // 2, LANES)

time: 1000 us -> 952 us (0.952)
  Pallas kernels: 714 us -> 669 us
    pallas_call x1, Pallas kernels: 98.5 us -> 67.9 us  [weighted_sums(): pl.pallas_call(functools.partial(sum_kernel, n_y, n_x), out_shape=(jax.Sh...]
    pallas_call x3 -> x2, Pallas kernels: 145 us -> 131 us  [run_experts(): pl.pallas_call(functools.partial(expert_kernel, k, n_chunk, first), out_s...]
    all_gather x3 -> x2, waiting for transfers between devices: 208 us -> 208 us  [local_step(): lax.all_gather(x3[bounds[k]:bounds[k + 1]], dev_axes, tiled=True)]
  transfers between devices with their start and end apart: 8 -> 7, of which waited for: 4 -> 2; matrix products, arithmetic and copies ran while one was open for 2% -> 1% of each run, Pallas kernels for 48% -> 49%
where the time goes in v4:
time: 952 us; the launch traced here: 940 us
  Pallas kernels  669 us (70%)
  waiting for transfers between devices  217 us (23%)
  between operations  21.5 us (2%)
  local copies, waits for them, and re-layouts  17.7 us (2%)
    pallas_call x1, Pallas kernels, spread(): pl.pallas_call(functools.partial(spread_kernel, rows_a, rows_b, n_y, n_x)...  262 us
    all_gather x2, waiting for transfers between devices, local_step(): lax.all_gather(x3[bounds[k]:bounds[k + 1]], dev_axes, tiled=True)  208 us
    pallas_call x1, Pallas kernels, reduce_back(): pl.pallas_call(functools.partial(reduce_kernel, n_y, n_x), out_shape=jax....  145 us
    pallas_call x2, Pallas kernels, run_experts(): pl.pallas_call(functools.partial(expert_kernel, k, n_chunk, first), out_s...  131 us
    pallas_call x1, Pallas kernels, weighted_sums(): pl.pallas_call(functools.partial(sum_kernel, n_y, n_x), out_shape=(jax.Sh...  67.9 us
    pallas_call x1, Pallas kernels, build_lists(): pl.pallas_call(functools.partial(list_kernel, cap, slots_a, slots_b, boun...  34.5 us
    pallas_call x1, Pallas kernels, route(): pl.pallas_call(functools.partial(route_kernel, bounds), out_shape=(jax.Sh...  28.4 us
  transfers between devices with their start and end apart: 7, of which 2 were waited for; matrix products, arithmetic and copies ran while one was open for 1% of the time, Pallas kernels for 49%

profile of v4, /device:TPU:107, one launch (start us, length us, event | category | flops | bytes accessed | tf_op | source)
XLA Modules:
  0.0 939.9 jit_solution(2727834412690194014)
XLA Ops:
  6.6 2.2 slice_bitcast_fusion
  8.7 2.8 copy.29
  11.5 0.1 all-gather.7.cloned.1.call-update
  11.6 0.1 all-gather.5.cloned.1.call-start
  11.6 1.2 slice_bitcast_fusion.1
  12.9 1.2 copy.28
  14.0 0.1 all-gather.5.cloned.1.call-update
  14.1 0.7 collective-permute-start
  14.8 0.1 collective-permute-start.1
  14.9 0.0 copy-done.5
  14.9 1.0 copy.21.ids_ref
  15.9 1.0 copy.22.gate_ref
  16.9 28.4 %route.1 = (s32[128,128]{1,0:T(8,128)}, f32[128,128]{1,0:T(8,128)}, s32[8,128]{1,0:T(8,128)}) custom-call(s32[1024,8]{1,0:T(8,128)} %copy.21.ids_ref, f32[1024,8]{1,0:T(8,128)} %copy.22.gate_ref), custom_call_target="tpu_custom_call" | custom-call | flops 20000000000 | bytes 1000000 | tf_op jit(solution)/shard_map/route/pallas_call | solution.py:79
  45.3 0.8 broadcast_in_dim.19
  46.2 0.7 broadcast_in_dim.20
  46.9 0.7 pad_add_fusion
  47.6 7.4 all-to-all-start
  55.0 0.1 all-gather.11.cloned.1.call-start
  55.1 0.6 pad_add_fusion.1.place_ref.refs_6_.place
  55.7 9.3 all-to-all-done
  65.0 0.0 copy-start.1
  65.0 0.1 reduce_window_sum.13
  65.1 1.5 fusion.3
  66.6 34.5 %row_lists.1 = (s32[16448]{0:T(1024)}, s32[256]{0:T(256)}, s32[256]{0:T(256)}, s32[256]{0:T(256)}, s32[256]{0:T(256)}, /*index=5*/s32[24]{0:T(128)}) custom-call(s32[2]{0:T(128)} %pad_add_fusion.1.place_ref.refs_6_.place, s32[65536]{0:T(1024)} %bitcast.43), custom_call_target="tpu_custom_call" | custom-call | flops 20000000000 | bytes 1000000 | tf_op jit(solution)/shard_map/row_lists/pallas_call | solution.py:176
  101.2 0.0 collective-permute-done.refs_9_
  101.2 0.0 collective-permute-done.1.refs_11_
  101.2 207.8 %all-gather.7.cloned.1.call-done.refs_7_ = bf16[25600,16,128]{2,1,0:T(8,128)(2,1)} async-done(((bf16[800,16,128]{2,1,0:T(8,128)(2,1)}), bf16[25600,16,128]{2,1,0:T(8,128)(2,1)}) %all-gather.7.cloned.1.call-update) | async-done | bytes 104857616 | tf_op jit(solution)/shard_map/all_gather | solution.py:742
  309.1 92.1 %experts.2 = (bf16[16384,8,128]{2,1,0:T(8,128)(2,1)}, bf16[16384,8,128]{2,1,0:T(8,128)(2,1)}) custom-call(s32[16448]{0:T(1024)} %get-tuple-element.87.refs_0_, s32[256]{0:T(256)} %get-tuple-element.88.refs_1_, s32[256]{0:T(256)} %get-tuple-element.89.refs_2_, s32[256]{0:T(256)} %get-tuple-element.90.refs_3_, s32[256]{0:T(256)} %get-tuple-element.91.refs_4_, ...), custom_call_target="tpu_custom_call" | custom-call | flops 161061273600 | bytes 60000000 | tf_op jit(solution)/shard_map/experts/pallas_call | solution.py:350
  401.1 0.1 all-gather.11.cloned.1.call-update
  401.2 0.1 all-gather.9.cloned.1.call-start
  401.3 0.3 reduce_window_sum.14
  401.7 0.0 copy-done.2
  401.7 0.3 squeeze.5
  402.0 1.2 fusion.6
  403.2 0.6 reduce_max.18
  403.9 0.7 reduce_max.19
  412.7 0.7 reshape.45.kept_b
  413.4 0.6 reshape.44.kept_a
  414.0 0.1 all-gather.9.cloned.1.call-update
  414.1 0.0 all-gather.5.cloned.1.call-done.refs_7_
  414.1 39.0 %experts.3 = (bf16[16384,8,128]{2,1,0:T(8,128)(2,1)}, bf16[16384,8,128]{2,1,0:T(8,128)(2,1)}) custom-call(s32[16448]{0:T(1024)} %get-tuple-element.87.refs_0_, s32[256]{0:T(256)} %get-tuple-element.88.refs_1_, s32[256]{0:T(256)} %get-tuple-element.89.refs_2_, s32[256]{0:T(256)} %get-tuple-element.90.refs_3_, ...), custom_call_target="tpu_custom_call", output_to_operand_aliasing={{0}: (12, {}), {1}: (13, {})} | custom-call | flops 45097156608 | bytes 60000000 | tf_op jit(solution)/shard_map/experts/pallas_call | solution.py:350
  453.2 262.1 %conditional.1 = (bf16[4,4096,8,128]{3,2,1,0:T(8,128)(2,1)}, bf16[4,4096,8,128]{3,2,1,0:T(8,128)(2,1)}) conditional(s32[]{:T(128)} %clamp.3, (bf16[4,4096,8,128]{3,2,1,0:T(8,128)(2,1)}, bf16[4,4096,8,128]{3,2,1,0:T(8,128)(2,1)}) %tuple.62, (bf16[4,4096,8,128]{3,2,1,0:T(8,128)(2,1)}, ...), branch_computations={%region_5.6_spmd, %region_6.7_spmd, %region_7.8_spmd, %region_8.9_... | conditional | bytes 16 | solution.py:783
  453.2 261.8 %spread_2688_2688.1 = (bf16[4,4096,8,128]{3,2,1,0:T(8,128)(2,1)}, bf16[4,4096,8,128]{3,2,1,0:T(8,128)(2,1)}, bf16[4096,8,128]{2,1,0:T(8,128)(2,1)}, bf16[4096,8,128]{2,1,0:T(8,128)(2,1)}) custom-call(bf16[4,4096,8,128]{3,2,1,0:T(8,128)(2,1)} %get-tuple-element.37.send_a, bf16[4,4096,8,128]{3,2,1,0:T(8,128)(2,1)} %get-tuple-element.38.send_b), custom_call_target="tpu_custom_call" | custom-call | tf_op jit(solution)/shard_map/cond/branch_1_fun/spread_2688_2688/pallas_call | solution.py:453
  715.2 0.0 all-gather.11.cloned.1.call-done.wgt_hbm
  715.3 0.0 all-gather.9.cloned.1.call-done.tok_hbm
  715.3 67.9 %weighted_sums.1 = (f32[4,1024,8,128]{3,2,1,0:T(8,128)}, f32[4,1024,8,128]{3,2,1,0:T(8,128)}) custom-call(s32[128]{0:T(128)} %reshape.44.kept_a, s32[128]{0:T(128)} %reshape.45.kept_b, s32[2]{0:T(128)} %pad_add_fusion.1.place_ref.refs_6_.place, s32[524288]{0:T(1024)} %all-gather.9.cloned.1.call-done.tok_hbm, f32[524288]{0:T(1024)} %all-gather.11.cloned.1.call-done.wgt_hbm, ...), custom_call_target="tpu_custom_call" | custom-call | flops 20000000000 | bytes 60000000 | tf_op jit(solution)/shard_map/weighted_sums/pallas_call | solution.py:592
  783.2 145.4 %reduce_back.1 = bf16[1024,2048]{1,0:T(8,128)(2,1)} custom-call(f32[4,1024,8,128]{3,2,1,0:T(8,128)} %get-tuple-element.107.z_a, f32[4,1024,8,128]{3,2,1,0:T(8,128)} %get-tuple-element.108.z_b, bf16[1024,2048]{1,0:T(8,128)(2,1)} %x_ref.1), custom_call_target="tpu_custom_call" | custom-call | tf_op jit(solution)/shard_map/reduce_back/pallas_call | solution.py:704
  928.6 4.8 copy.57
  (16 shorter events, 0.1 us)
Async XLA Ops:
  6.5 8.4 copy-start.5
  6.5 9.4 copy-start.6
  6.6 302.5 %all-gather.7.cloned.1.call-start = ((), (), s32[]{:S(2)}) async-start(), calls=%async_computation.2 | async-start | bytes 108134400 | tf_op jit(solution)/shard_map/all_gather | solution.py:742
  11.6 402.5 %all-gather.5.cloned.1.call-start = ((), (), s32[]{:S(2)}) async-start(), calls=%async_computation.1 | async-start | bytes 30277632 | tf_op jit(solution)/shard_map/all_gather | solution.py:742
  14.1 87.1 %collective-permute-start = (bf16[4,2048,768]{2,1,0:T(8,128)(2,1)}, bf16[4,2048,768]{2,1,0:T(8,128)(2,1)}, u32[]{:S(2)}, u32[]{:S(2)}) collective-permute-start(bf16[4,2048,768]{2,1,0:T(8,128)(2,1)} %refs_8_.3), channel_id=1, source_target_pairs={{0,1},{1,0},{2,3},{3,2},{4,5},{5,4},{6,7},{7,6},{8,9},{9,8},{10,11... | collective-permute-start | bytes 37748744 | tf_op jit(solution)/shard_map/ppermute | solution.py:744
  14.8 86.4 %collective-permute-start.1 = (bf16[4,768,2048]{2,1,0:T(8,128)(2,1)}, bf16[4,768,2048]{2,1,0:T(8,128)(2,1)}, u32[]{:S(2)}, u32[]{:S(2)}) collective-permute-start(bf16[4,768,2048]{2,1,0:T(8,128)(2,1)} %refs_10_.3), channel_id=1, source_target_pairs={{0,1},{1,0},{2,3},{3,2},{4,5},{5,4},{6,7},{7,6},{8,9},{9,8},{10,11... | collective-permute-start | bytes 37748744 | tf_op jit(solution)/shard_map/ppermute | solution.py:745
  47.6 17.4 %all-to-all-start = ((s32[32,16,128]{2,1,0:T(8,128)}), s32[32,16,128]{2,1,0:T(8,128)S(1)}, u32[]{:S(2)}, u32[]{:S(2)}) async-start(s32[32,16,128]{2,1,0:T(8,128)} %pad_add_fusion), calls=%async_computation | async-start | bytes 524288 | tf_op jit(solution)/shard_map/all_to_all | solution.py:752
  55.0 660.2 %all-gather.11.cloned.1.call-start = ((), (), s32[]{:S(2)}) async-start(), calls=%async_computation.4 | async-start | bytes 2162688 | tf_op jit(solution)/shard_map/all_gather | solution.py:774
  65.0 1.7 copy-start
  65.0 36.2 %copy-start.1 = (s32[32,1,128]{2,1,0:T(1,128)}, s32[32,1,128]{2,1,0:T(1,128)S(1)}, u32[]{:S(2)}) copy-start(s32[32,1,128]{2,1,0:T(1,128)S(1)} %slice.20) | copy-start | bytes 49156
  65.1 36.1 %copy-start.3 = (s32[32,128]{1,0:T(8,128)}, s32[32,128]{1,0:T(8,128)S(1)}, u32[]{:S(2)}) copy-start(s32[32,128]{1,0:T(8,128)S(1)} %reduce_window_sum.13) | copy-start | bytes 49156
  309.1 92.3 %copy-start.4 = (s32[32,128]{1,0:T(8,128)S(1)}, s32[32,128]{1,0:T(8,128)}, u32[]{:S(2)}) copy-start(s32[32,128]{1,0:T(8,128)} %copy-done.3) | copy-start | bytes 49156
  309.1 92.6 %copy-start.2 = (s32[32,1,128]{2,1,0:T(1,128)S(1)}, s32[32,1,128]{2,1,0:T(1,128)}, u32[]{:S(2)}) copy-start(s32[32,1,128]{2,1,0:T(1,128)} %copy-done.1) | copy-start | bytes 49156
  401.2 314.1 %all-gather.9.cloned.1.call-start = ((), (), s32[]{:S(2)}) async-start(), calls=%async_computation.3 | async-start | bytes 2162688 | tf_op jit(solution)/shard_map/all_gather | solution.py:773
Sparse Core Ops, SparseCore 0:
  11.7 297.3 all-gather.6
  311.1 96.9 all-gather.4
  410.2 41.7 all-gather.10
  453.9 40.3 all-gather.8
